TPU v7x, 32 devices: a whole 2x2x4 slice. The times are simulated.
32 devices in a mesh: elem: 16 (over z, y, core), band: 2 (over x).
Axes of the slice: x: 2, y: 2, z: 4, core: 2. Of those that a mesh axis runs over, the one named last changes fastest.
Arguments:
- y_current: bfloat16 [512, 64, 512], P('elem', None, 'band'), may hold values from -6 to 6
- y_previous: bfloat16 [512, 64, 512], P('elem', None, 'band'), may hold values from -6 to 6
- h_blocks: bfloat16 [512, 64, 320], P('elem'), may hold values from -0.3125 to 0.3125
- basis_sizes: int32 [512], P('elem'), may hold values from 40 to 64
- neighbours: int32 [512, 4], P('elem'), may hold values from 0 to 511, as said below
Outputs:
- filtered: bfloat16 [512, 64, 512], P('elem', None, 'band')
- margin: float32 [512, 512], P('elem', 'band')
Inputs may be any that keep to these rules, and one draw needn't show every extreme that they name: `neighbours`: the elements lie on a periodic grid of 32 x 16; row i lists the elements that share an edge with element i, in the order previous grid row, next grid row, previous column, next column, so adjacency is symmetric. Element g belongs to index g // 32 of elem, whose elements fill 2 consecutive grid rows in some order; a neighbour therefore belongs to the same index or to one of the two beside it, periodically, and exactly 16 of an index's elements have a neighbour on the next index, and 16 on the previous one.
All inputs are finite; a program needn't handle non-finite values.
Results may differ from a plain program's by a relative error of at most 0.018.
Values may be sent and summed in bfloat16 or wider, within the bound.
No kernel may reach another device: no remote copies, remote signals or barrier semaphores. Data moves between devices by JAX's collectives and lax.ppermute only.
A program may use at most 64 MiB of HBM per device.

v0:
```python
import jax
import jax.numpy as jnp
from jax import lax
from jax.sharding import PartitionSpec as P

BMAX = 64
GY = 16
DEGREES = 2


center_value = 0.3
spectral_half = 1.7


def shifted(block, axis, distance):
    devices = range(lax.axis_size(axis))
    route = [((i - distance) % len(devices), i) for i in devices]
    return lax.ppermute(block, axis, route)


def referenced_slots(relative, local_index, wanted, local_count):
    positions = jnp.arange(local_count, dtype=jnp.int32)
    marked = jnp.where(relative == wanted, local_index, -1)
    present = jnp.any(marked[:, :, None] == positions[None, None, :], axis=(0, 1))
    return jnp.cumsum(present.astype(jnp.int32)) - 1


def on_device(y_current, y_previous, h_blocks, basis_sizes, neighbours):
    local_count = neighbours.shape[0]
    band_width = y_current.shape[2]
    count_elem = lax.axis_size("elem")
    myself = lax.axis_index("elem")
    owners = neighbours // local_count
    local_index = neighbours % local_count
    relative = (owners - myself + 1) % count_elem - 1
    send_next = jnp.nonzero(jnp.any(relative == 1, axis=1), size=GY)[0]
    send_prev = jnp.nonzero(jnp.any(relative == -1, axis=1), size=GY)[0]
    slot_prev = referenced_slots(relative, local_index, -1, local_count)
    slot_next = referenced_slots(relative, local_index, 1, local_count)
    pool_index = jnp.where(
        relative == 0,
        local_index,
        jnp.where(
            relative == -1,
            local_count + jnp.take(slot_prev, local_index),
            local_count + GY + jnp.take(slot_next, local_index),
        ),
    )
    row_mask = (jnp.arange(BMAX, dtype=jnp.int32)[None, :] < basis_sizes[:, None]).astype(
        jnp.bfloat16
    )[:, :, None]
    mask_float = row_mask.astype(jnp.float32)
    current = y_current * row_mask
    previous = y_previous * row_mask
    for degree in range(DEGREES):
        from_prev = shifted(current[send_next], "elem", 1)
        from_next = shifted(current[send_prev], "elem", -1)
        pool = jnp.concatenate([current, from_prev, from_next], axis=0)
        nearby = pool[pool_index]
        stacked = jnp.concatenate([current[:, None], nearby], axis=1).reshape(
            local_count, 5 * BMAX, band_width
        )
        applied = jnp.einsum("irc,icb->irb", h_blocks, stacked, preferred_element_type=jnp.float32)
        following = mask_float * (
            2.0 / spectral_half * (applied - center_value * current.astype(jnp.float32))
            - previous.astype(jnp.float32)
        )
        previous = current
        current = following.astype(jnp.bfloat16)
    flat = current.reshape(local_count * BMAX, band_width)
    gathered = lax.all_gather(flat, "band", axis=1, tiled=True)
    summed = lax.psum_scatter(
        lax.dot_general(
            gathered, flat, (((0,), (0,)), ((), ())), preferred_element_type=jnp.float32
        ).astype(jnp.bfloat16),
        "elem",
        scatter_dimension=0,
        tiled=True,
    ).astype(jnp.float32)
    margin = summed / jnp.float32(local_count * count_elem * BMAX)
    return (current, margin)


def solution(mesh):
    in_specs = (
        P("elem", None, "band"),
        P("elem", None, "band"),
        P("elem", None, None),
        P("elem"),
        P("elem", None),
    )
    out_specs = (P("elem", None, "band"), P("elem", "band"))
    return jax.shard_map(
        on_device, mesh=mesh, in_specs=in_specs, out_specs=out_specs, check_vma=False
    )
```

profile of v0, /device:TPU:0, one launch (start us, length us, event | category | flops | bytes accessed | tf_op | source)
XLA Modules:
  0.0 174.4 jit_solution(13674862233385489575)
XLA Ops:
  7.2 0.0 copy-start
  7.2 0.0 all-gather.2.cloned.1.call-start
  7.2 0.9 copy.31
  8.2 0.1 reduce_or.36
  8.3 0.6 convert_reduce_fusion.1
  8.9 0.7 fusion.27
  9.6 0.1 copy.35
  9.7 0.1 reduce-window.30
  9.8 0.1 fusion.14
  9.9 0.8 scatter_custom_fusion
  10.7 0.1 copy.36
  10.8 0.8 fusion.25
  11.6 1.6 broadcast_multiply_fusion
  13.1 0.6 gather_fusion
  13.7 0.5 collective-permute-start
  14.3 0.1 fusion.32
  14.4 0.6 convert_reduce_fusion
  15.0 0.1 copy.37
  15.1 0.1 reduce-window.31
  15.2 0.1 fusion.15
  15.3 0.8 scatter_custom_fusion.1
  16.1 0.1 copy.38
  16.2 0.8 fusion.26
  17.0 1.4 gather_fusion.1
  18.4 5.0 %collective-permute-start.1 = (bf16[16,64,256]{2,1,0:T(8,128)(2,1)}, bf16[16,64,256]{2,1,0:T(8,128)(2,1)}, u32[]{:S(2)}, u32[]{:S(2)}) collective-permute-start(bf16[16,64,256]{2,1,0:T(8,128)(2,1)} %gather_fusion.1), channel_id=1, source_target_pairs={{2,0},{4,2},{6,4},{8,6},{10,8},{12,10},{14,12},{16,14},{18,16},{20... | collective-permute-start | bytes 1572872 | tf_op jit(solution)/shard_map/ppermute | solution.py:18
  23.4 0.1 copy.39
  23.4 0.1 fusion.8
  23.6 0.1 copy.40
  23.6 0.1 reduce-window.32
  23.7 0.1 add_reduce_fusion.1
  23.8 0.1 copy.41
  23.9 0.1 fusion.9
  24.0 0.1 reshape.406
  24.1 1.2 gather_fusion.6
  25.4 0.1 reshape.409
  25.5 0.1 copy.42
  25.6 0.1 reduce-window.33
  25.6 0.1 add_reduce_fusion
  25.7 1.2 gather_fusion.7
  27.0 0.1 reshape.413
  27.1 0.1 reshape.352
  27.2 2.5 %fusion.40 = bf16[32,1,64,256]{3,2,1,0:T(8,128)(2,1)} fusion(bf16[32,64,256]{2,1,0:T(8,128)(2,1)} %param.7, bf16[32,64]{1,0:T(8,128)(2,1)S(1)} %get-tuple-element.9), kind=kLoop, calls=%fused_computation.97 | loop fusion | flops 524288 | bytes 2101248 | tf_op jit(solution)/shard_map/broadcast_in_dim | solution.py:60
  29.8 0.0 collective-permute-done
  29.8 0.6 collective-permute-done.1
  30.4 2.8 %pad_maximum_fusion.2 = bf16[64,64,256]{2,1,0:T(8,128)(2,1)} fusion(bf16[16,64,256]{2,1,0:T(8,128)(2,1)} %collective-permute-done.1, bf16[16,64,256]{2,1,0:T(8,128)(2,1)} %collective-permute-done, bf16[32,64,256]{2,1,0:T(8,128)(2,1)S(1)} %broadcast_multiply_fusion), kind=kLoop, calls=%fused_computation.21 | loop fusion | flops 2097152 | bytes 4194304 | tf_op jit(solution)/shard_map/concatenate | solution.py:58
  33.1 4.3 %gather_fusion.2 = bf16[128,64,256]{2,1,0:T(8,128)(2,1)} fusion(bf16[64,64,256]{2,1,0:T(8,128)(2,1)} %pad_maximum_fusion.2, s32[1024]{0:T(1024)S(1)} %pad_clamp_fusion), kind=kCustom, calls=%fused_computation.4 | custom fusion | bytes 8389120 | tf_op jit(solution)/shard_map/gather | solution.py:59
  37.5 3.0 %pad_maximum_fusion = bf16[32,5,64,256]{3,2,1,0:T(8,128)(2,1)S(1)} fusion(bf16[32,4,64,256]{3,2,1,0:T(8,128)(2,1)} %bitcast.39, bf16[32,1,64,256]{3,2,1,0:T(8,128)(2,1)} %fusion.40), kind=kLoop, calls=%fused_computation.10 | loop fusion | flops 2621440 | bytes 10485760 | tf_op jit(solution)/shard_map/concatenate | solution.py:60
  40.5 2.3 %fusion.4 = bf16[32,64,256]{2,1,0:T(8,128)(2,1)} fusion(bf16[32,64,256]{2,1,0:T(8,128)(2,1)S(1)} %broadcast_multiply_fusion, bf16[32,64,320]{2,1,0:T(8,128)(2,1)S(1)} %copy-done, bf16[32,320,256]{2,1,0:T(8,128)(2,1)S(1)} %bitcast.37, bf16[32,64,256]{2,1,0:T(8,128)(2,1)S(1)} %copy-done.2, f32[32,64]{1,0:T(8,128)S(1)} %get-tuple-element.8, ...), kind=kOutput, calls=%fused_computation.18 | convolution fusion | flops 340262912 | bytes 9711616 | tf_op jit(solution)/shard_map/irc,icb->irb/dot_general | solution.py:63
  42.9 1.8 %gather_fusion.4 = bf16[16,64,256]{2,1,0:T(8,128)(2,1)S(1)} fusion(bf16[32,64,256]{2,1,0:T(8,128)(2,1)} %fusion.4, s32[1024]{0:T(1024)S(1)} %pad_clamp_fusion.2), kind=kCustom, calls=%fused_computation.6 | custom fusion | bytes 1048640 | tf_op jit(solution)/shard_map/gather | solution.py:57
  44.7 2.6 %gather_fusion.3 = bf16[16,64,256]{2,1,0:T(8,128)(2,1)} fusion(bf16[32,64,256]{2,1,0:T(8,128)(2,1)} %fusion.4, s32[1024]{0:T(1024)S(1)} %pad_clamp_fusion.3), kind=kCustom, calls=%fused_computation.5 | custom fusion | bytes 1048640 | tf_op jit(solution)/shard_map/gather | solution.py:56
  47.3 1.3 collective-permute-start.2
  48.6 3.3 %collective-permute-start.3 = (bf16[16,64,256]{2,1,0:T(8,128)(2,1)S(1)}, bf16[16,64,256]{2,1,0:T(8,128)(2,1)S(1)}, u32[]{:S(2)}, u32[]{:S(2)}) collective-permute-start(bf16[16,64,256]{2,1,0:T(8,128)(2,1)S(1)} %gather_fusion.4), channel_id=1, source_target_pairs={{2,0},{4,2},{6,4},{8,6},{10,8},{12,10},{14,12},{16,14},{18,16},{20... | collective-permute-start | bytes 1572872 | tf_op jit(solution)/shard_map/ppermute | solution.py:18
  51.9 7.2 %collective-permute-done.2 = bf16[16,64,256]{2,1,0:T(8,128)(2,1)S(1)} collective-permute-done((bf16[16,64,256]{2,1,0:T(8,128)(2,1)}, bf16[16,64,256]{2,1,0:T(8,128)(2,1)S(1)}, u32[]{:S(2)}, u32[]{:S(2)}) %collective-permute-start.2) | collective-permute-done | bytes 524320 | tf_op jit(solution)/shard_map/ppermute | solution.py:18
  59.1 2.8 %pad_maximum_fusion.3 = bf16[64,64,256]{2,1,0:T(8,128)(2,1)} fusion(bf16[16,64,256]{2,1,0:T(8,128)(2,1)S(1)} %collective-permute-done.3, bf16[16,64,256]{2,1,0:T(8,128)(2,1)S(1)} %collective-permute-done.2, bf16[32,64,256]{2,1,0:T(8,128)(2,1)} %fusion.4), kind=kLoop, calls=%fused_computation.22 | loop fusion | flops 2097152 | bytes 4194304 | tf_op jit(solution)/shard_map/concatenate | solution.py:58
  61.8 4.3 %gather_fusion.5 = bf16[128,64,256]{2,1,0:T(8,128)(2,1)} fusion(bf16[64,64,256]{2,1,0:T(8,128)(2,1)} %pad_maximum_fusion.3, s32[1024]{0:T(1024)S(1)} %pad_clamp_fusion), kind=kCustom, calls=%fused_computation.7 | custom fusion | bytes 8389120 | tf_op jit(solution)/shard_map/gather | solution.py:59
  66.2 3.0 %pad_maximum_fusion.1 = bf16[32,5,64,256]{3,2,1,0:T(8,128)(2,1)S(1)} fusion(bf16[32,4,64,256]{3,2,1,0:T(8,128)(2,1)} %bitcast.40, bf16[32,1,64,256]{3,2,1,0:T(8,128)(2,1)} %bitcast.36), kind=kLoop, calls=%fused_computation.11 | loop fusion | flops 2621440 | bytes 10485760 | tf_op jit(solution)/shard_map/concatenate | solution.py:60
  69.2 2.3 %fusion.6 = bf16[32,64,256]{2,1,0:T(8,128)(2,1)} fusion(bf16[32,64,256]{2,1,0:T(8,128)(2,1)S(1)} %broadcast_multiply_fusion, bf16[32,64,256]{2,1,0:T(8,128)(2,1)S(1)} %copy-done.1, bf16[32,64,320]{2,1,0:T(8,128)(2,1)S(1)} %copy-done, bf16[32,320,256]{2,1,0:T(8,128)(2,1)S(1)} %bitcast.38, f32[32,64]{1,0:T(8,128)S(1)} %get-tuple-element.8), kind=kOutput, calls=%fused_computation.20 | convolution fusion | flops 339738624 | bytes 9707520 | tf_op jit(solution)/shard_map/irc,icb->irb/dot_general | solution.py:63
  71.5 0.0 all-gather.2.cloned.1.call-update
  71.5 0.0 reduce-scatter.2.cloned.1.call-start
  71.6 35.4 %all-gather.2.cloned.1.call-done = bf16[2048,512]{1,0:T(8,128)(2,1)} async-done(((bf16[2048,256]{1,0:T(8,128)(2,1)}), bf16[2048,512]{1,0:T(8,128)(2,1)}) %all-gather.2.cloned.1.call-update) | async-done | bytes 2097168 | tf_op jit(solution)/shard_map/all_gather | solution.py:71
  107.0 3.3 %convolution_convert_fusion = bf16[512,256]{1,0:T(8,128)(2,1)} fusion(bf16[2048,512]{1,0:T(8,128)(2,1)} %all-gather.2.cloned.1.call-done, bf16[2048,256]{1,0:T(8,128)(2,1)} %bitcast.42), kind=kOutput, calls=%fused_computation.25 | convolution fusion | flops 537001984 | bytes 3407872 | tf_op jit(solution)/shard_map/dot_general | solution.py:73
  110.3 0.0 reduce-scatter.2.cloned.1.call-update
  110.3 55.9 %reduce-scatter.2.cloned.1.call-done = bf16[32,256]{1,0:T(8,128)(2,1)} async-done(((bf16[512,256]{1,0:T(8,128)(2,1)}), bf16[32,256]{1,0:T(8,128)(2,1)}) %reduce-scatter.2.cloned.1.call-update) | async-done | bytes 16400 | tf_op jit(solution)/shard_map/reduce_scatter | solution.py:72
  166.2 1.3 convert_multiply_fusion.1
  (20 shorter events, 0.2 us)
Async XLA Ops:
  7.2 33.3 %copy-start = (bf16[32,64,320]{2,1,0:T(8,128)(2,1)S(1)}, bf16[32,64,320]{2,1,0:T(8,128)(2,1)}, u32[]{:S(2)}) copy-start(bf16[32,64,320]{2,1,0:T(8,128)(2,1)} %param.9) | copy-start | bytes 3932164
  7.2 99.8 %all-gather.2.cloned.1.call-start = ((), (), s32[]{:S(2)}) async-start(), calls=%async_computation.1 | async-start | bytes 3145728 | tf_op jit(solution)/shard_map/all_gather | solution.py:71
  13.7 16.0 %collective-permute-start = (bf16[16,64,256]{2,1,0:T(8,128)(2,1)S(1)}, bf16[16,64,256]{2,1,0:T(8,128)(2,1)}, u32[]{:S(2)}, u32[]{:S(2)}) collective-permute-start(bf16[16,64,256]{2,1,0:T(8,128)(2,1)S(1)} %gather_fusion), channel_id=1, source_target_pairs={{30,0},{0,2},{2,4},{4,6},{6,8},{8,10},{10,12},{12,14},{14,16},{16,... | collective-permute-start | bytes 1572872 | tf_op jit(solution)/shard_map/ppermute | solution.py:18
  18.4 12.0 %collective-permute-start.1 = (bf16[16,64,256]{2,1,0:T(8,128)(2,1)}, bf16[16,64,256]{2,1,0:T(8,128)(2,1)}, u32[]{:S(2)}, u32[]{:S(2)}) collective-permute-start(bf16[16,64,256]{2,1,0:T(8,128)(2,1)} %gather_fusion.1), channel_id=1, source_target_pairs={{2,0},{4,2},{6,4},{8,6},{10,8},{12,10},{14,12},{16,14},{18,16},{20... | collective-permute-start | bytes 1572872 | tf_op jit(solution)/shard_map/ppermute | solution.py:18
  37.5 3.0 %copy-start.2 = (bf16[32,64,256]{2,1,0:T(8,128)(2,1)S(1)}, bf16[32,64,256]{2,1,0:T(8,128)(2,1)}, u32[]{:S(2)}) copy-start(bf16[32,64,256]{2,1,0:T(8,128)(2,1)} %param.8) | copy-start | bytes 3145732
  47.3 11.8 %collective-permute-start.2 = (bf16[16,64,256]{2,1,0:T(8,128)(2,1)}, bf16[16,64,256]{2,1,0:T(8,128)(2,1)S(1)}, u32[]{:S(2)}, u32[]{:S(2)}) collective-permute-start(bf16[16,64,256]{2,1,0:T(8,128)(2,1)} %gather_fusion.3), channel_id=1, source_target_pairs={{30,0},{0,2},{2,4},{4,6},{6,8},{8,10},{10,12},{12,14},{14,16},{16,... | collective-permute-start | bytes 1572872 | tf_op jit(solution)/shard_map/ppermute | solution.py:18
  48.6 10.5 %collective-permute-start.3 = (bf16[16,64,256]{2,1,0:T(8,128)(2,1)S(1)}, bf16[16,64,256]{2,1,0:T(8,128)(2,1)S(1)}, u32[]{:S(2)}, u32[]{:S(2)}) collective-permute-start(bf16[16,64,256]{2,1,0:T(8,128)(2,1)S(1)} %gather_fusion.4), channel_id=1, source_target_pairs={{2,0},{4,2},{6,4},{8,6},{10,8},{12,10},{14,12},{16,14},{18,16},{20... | collective-permute-start | bytes 1572872 | tf_op jit(solution)/shard_map/ppermute | solution.py:18
  66.2 3.0 %copy-start.1 = (bf16[32,64,256]{2,1,0:T(8,128)(2,1)S(1)}, bf16[32,64,256]{2,1,0:T(8,128)(2,1)}, u32[]{:S(2)}) copy-start(bf16[32,64,256]{2,1,0:T(8,128)(2,1)} %fusion.4) | copy-start | bytes 3145732
  71.5 94.7 %reduce-scatter.2.cloned.1.call-start = ((), (), s32[]{:S(2)}) async-start(), calls=%async_computation.2 | async-start | bytes 278528 | tf_op jit(solution)/shard_map/reduce_scatter | solution.py:72
Sparse Core Ops, SparseCore 0:
  71.7 35.2 all-gather.1
  110.5 55.7 reduce-scatter.1
where the time goes:
time: 175 us; the launch traced here: 174 us
  waiting for transfers between devices  99.1 us (57%)
  other arithmetic  23.4 us (13%)
  local copies, waits for them, and re-layouts  19.5 us (11%)
  between operations  14.2 us (8%)
  starting transfers between devices  10.2 us (6%)
  matrix products  7.97 us (5%)
    reduce_scatter x1, waiting for transfers between devices, on_device(): lax.psum_scatter(lax.dot_general(gathered, flat, (((0,), (0,)), ((), ()))...  55.9 us
    all_gather x1, waiting for transfers between devices, on_device(): gathered = lax.all_gather(flat, 'band', axis=1, tiled=True)  35.4 us
    ppermute x4, starting transfers between devices, shifted(): return lax.ppermute(block, axis, route)  10.2 us
    gather x2, local copies, waits for them, and re-layouts, on_device(): nearby = pool[pool_index]  8.66 us
    ppermute x4, waiting for transfers between devices, shifted(): return lax.ppermute(block, axis, route)  7.79 us
    concatenate x2, other arithmetic, on_device(): jnp.concatenate([current[:, None], nearby], axis=1)  6.05 us
    concatenate x2, other arithmetic, on_device(): pool = jnp.concatenate([current, from_prev, from_next], axis=0)  5.56 us
    dot_general x2, matrix products, on_device(): jnp.einsum('irc,icb->irb', h_blocks, stacked, preferred_element_type=jnp....  4.64 us
  transfers between devices with their start and end apart: 6, of which 4 were waited for; matrix products, arithmetic and copies ran while one was open for 6% of the time, Pallas kernels for 0%

commit v1 on v0

v1 whole, which is shorter than its diff:
```python
import jax
import jax.numpy as jnp
from jax import lax
from jax.experimental import pallas as pl
from jax.experimental.pallas import tpu as pltpu
from jax.sharding import PartitionSpec as P

GY = 16
DEGREES = 2

center_value = 0.3
spectral_half = 1.7

VM = pl.BlockSpec(memory_space=pltpu.VMEM)
SM = pl.BlockSpec(memory_space=pltpu.SMEM)


def shifted(block, axis, distance):
    count = lax.axis_size(axis)
    return lax.ppermute(block, axis, [((i - distance) % count, i) for i in range(count)])


def own_bases(local_count, count_elem):
    myself = lax.axis_index("elem")
    before = jnp.where(myself == 0, count_elem - 1, myself - 1)
    after = jnp.where(myself == count_elem - 1, 0, myself + 1)
    return before * local_count, myself * local_count, after * local_count


def within(value, base, local_count):
    return (value >= base) & (value < base + local_count)


def send_lists(near, orders, local_count, bases):
    base_prev, _, base_next = bases
    to_next = jnp.int32(0)
    to_prev = jnp.int32(0)
    for i in range(local_count):
        lower = within(near[i, 1], base_next, local_count)
        upper = within(near[i, 0], base_prev, local_count)
        orders[jnp.where(lower, to_next, 2 * GY)] = i
        orders[jnp.where(upper, GY + to_prev, 2 * GY)] = i
        to_next = to_next + lower.astype(jnp.int32)
        to_prev = to_prev + upper.astype(jnp.int32)


def row_index(block, width):
    return lax.broadcasted_iota(jnp.int32, (block, width), 0)


def pack(values, sizes, near, count_elem):
    local_count, block, width = values.shape

    def body(near, sizes, values, to_next, to_prev, orders):
        bases = own_bases(local_count, count_elem)
        send_lists(near, orders, local_count, bases)
        rows = row_index(block, width)
        for s in range(GY):
            for out, at in ((to_next, orders[s]), (to_prev, orders[GY + s])):
                held = values[at].astype(jnp.float32)
                out[s] = jnp.where(rows < sizes[at], held, 0.0).astype(jnp.bfloat16)

    halo = jax.ShapeDtypeStruct((GY, block, width), jnp.bfloat16)
    return pl.pallas_call(
        body,
        name="pack",
        in_specs=[SM, SM, VM],
        out_specs=[VM, VM],
        out_shape=[halo, halo],
        scratch_shapes=[pltpu.SMEM((2 * GY + 1,), jnp.int32)],
    )(near, sizes, values)


def tables(near, count_elem):
    local_count = near.shape[0]

    def body(near, pool_index, orders, slots, marks):
        bases = own_bases(local_count, count_elem)
        base_prev, base, base_next = bases
        send_lists(near, orders, local_count, bases)
        for j in range(2 * local_count):
            marks[j] = 0
        for i in range(local_count):
            upper = within(near[i, 0], base_prev, local_count)
            lower = within(near[i, 1], base_next, local_count)
            marks[jnp.where(upper, near[i, 0] - base_prev, 2 * local_count)] = 1
            marks[jnp.where(lower, local_count + near[i, 1] - base_next, 2 * local_count)] = 1
        from_prev = jnp.int32(local_count)
        from_next = jnp.int32(local_count + GY)
        for j in range(local_count):
            slots[j] = from_prev
            slots[local_count + j] = from_next
            from_prev = from_prev + marks[j]
            from_next = from_next + marks[local_count + j]
        for i in range(local_count):
            upper = within(near[i, 0], base_prev, local_count)
            lower = within(near[i, 1], base_next, local_count)
            far_prev = slots[jnp.where(upper, near[i, 0] - base_prev, 0)]
            far_next = slots[jnp.where(lower, local_count + near[i, 1] - base_next, 0)]
            pool_index[4 * i] = jnp.where(upper, far_prev, near[i, 0] - base)
            pool_index[4 * i + 1] = jnp.where(lower, far_next, near[i, 1] - base)
            pool_index[4 * i + 2] = near[i, 2] - base
            pool_index[4 * i + 3] = near[i, 3] - base

    return pl.pallas_call(
        body,
        name="tables",
        in_specs=[SM],
        out_specs=[SM, SM],
        out_shape=[
            jax.ShapeDtypeStruct((4 * local_count,), jnp.int32),
            jax.ShapeDtypeStruct((2 * GY + 1,), jnp.int32),
        ],
        scratch_shapes=[
            pltpu.SMEM((2 * local_count,), jnp.int32),
            pltpu.SMEM((2 * local_count + 1,), jnp.int32),
        ],
    )(near)


def degree_step(pool_index, orders, sizes, current, previous, from_prev, from_next, h_blocks, last):
    local_count, block, width = current.shape

    def body(pool_index, orders, sizes, current, previous, from_prev, from_next, h_blocks, following, *rest):
        pool = rest[-1]
        rows = row_index(block, width)
        for i in range(local_count):
            held = current[i].astype(jnp.float32)
            pool[i] = jnp.where(rows < sizes[i], held, 0.0).astype(jnp.bfloat16)
        pool[local_count : local_count + GY] = from_prev[...]
        pool[local_count + GY :] = from_next[...]
        for i in range(local_count):
            own = pool[i]
            stacked = jnp.concatenate(
                [own] + [pool[pool_index[4 * i + k]] for k in range(4)], axis=0
            )
            applied = jnp.dot(h_blocks[i], stacked, preferred_element_type=jnp.float32)
            value = 2.0 / spectral_half * (
                applied - center_value * own.astype(jnp.float32)
            ) - previous[i].astype(jnp.float32)
            following[i] = jnp.where(rows < sizes[i], value, 0.0).astype(jnp.bfloat16)
        if not last:
            to_next, to_prev = rest[:2]
            for s in range(GY):
                to_next[s] = following[orders[s]]
                to_prev[s] = following[orders[GY + s]]

    whole = jax.ShapeDtypeStruct(current.shape, jnp.bfloat16)
    halo = jax.ShapeDtypeStruct((GY, block, width), jnp.bfloat16)
    outs = [whole] if last else [whole, halo, halo]
    return pl.pallas_call(
        body,
        name="degree_last" if last else "degree",
        in_specs=[SM, SM, SM] + [VM] * 5,
        out_specs=[VM] * len(outs),
        out_shape=outs,
        scratch_shapes=[pltpu.VMEM((local_count + 2 * GY, block, width), jnp.bfloat16)],
    )(pool_index, orders, sizes, current, previous, from_prev, from_next, h_blocks)


def gram(left, right):
    return lax.dot_general(
        left, right, (((0,), (0,)), ((), ())), preferred_element_type=jnp.float32
    ).astype(jnp.bfloat16)


def on_device(y_current, y_previous, h_blocks, basis_sizes, neighbours):
    local_count, block, band_width = y_current.shape
    count_elem = lax.axis_size("elem")
    count_band = lax.axis_size("band")
    current, previous = y_current, y_previous
    to_next, to_prev = pack(current, basis_sizes, neighbours, count_elem)
    pool_index, orders = tables(neighbours, count_elem)
    for degree in range(DEGREES):
        from_prev = shifted(to_next, "elem", 1)
        from_next = shifted(to_prev, "elem", -1)
        last = degree == DEGREES - 1
        result = degree_step(
            pool_index, orders, basis_sizes, current, previous, from_prev, from_next, h_blocks, last
        )
        previous = current
        current = result[0]
        if not last:
            to_next, to_prev = result[1:]
    flat = current.reshape(local_count * block, band_width)
    band = lax.axis_index("band")
    parts = [gram(flat, flat)]
    for step in range(1, count_band):
        parts.append(gram(shifted(flat, "band", step), flat))
    if count_band == 2:
        ordered = jnp.stack(
            [jnp.where(band == 0, parts[0], parts[1]), jnp.where(band == 0, parts[1], parts[0])]
        )
    else:
        ordered = jnp.stack(parts)[(band - jnp.arange(count_band)) % count_band]
    rows = count_band * band_width // count_elem
    pieces = ordered.reshape(count_elem, rows, band_width)
    landed = lax.all_to_all(pieces, "elem", 0, 0)
    summed = jnp.sum(landed.astype(jnp.float32), axis=0)
    margin = summed / jnp.float32(local_count * count_elem * block)
    return (current, margin)


def solution(mesh):
    in_specs = (
        P("elem", None, "band"),
        P("elem", None, "band"),
        P("elem", None, None),
        P("elem"),
        P("elem", None),
    )
    out_specs = (P("elem", None, "band"), P("elem", "band"))
    return jax.shard_map(
        on_device, mesh=mesh, in_specs=in_specs, out_specs=out_specs, check_vma=False
    )
```

time: 175 us -> 85.7 us (0.49)
  waiting for transfers between devices: 99.1 us -> 32 us
  other arithmetic: 23.4 us -> 0.69 us
  blocking collectives: 0 us -> 19.6 us
  local copies, waits for them, and re-layouts: 19.5 us -> 3.23 us
  Pallas kernels: 0 us -> 14.8 us
  between operations: 14.2 us -> 0.68 us
  matrix products: 7.97 us -> 2.19 us
  starting transfers between devices: 10.2 us -> 12.1 us
    reduce_scatter x1 -> x0, waiting for transfers between devices: 55.9 us -> none  [on_device(): lax.psum_scatter(lax.dot_general(gathered, flat, (((0,), (0,)), ((), ()))...]
    all_gather x1 -> x0, waiting for transfers between devices: 35.4 us -> none  [on_device(): gathered = lax.all_gather(flat, 'band', axis=1, tiled=True)]
    ppermute x4 -> x5, waiting for transfers between devices: 7.79 us -> 32 us  [shifted(): lax.ppermute(block, axis, [((i - distance) % count, i) for i in range(cou...]
    all_to_all x0 -> x1, blocking collectives: none -> 19.6 us  [on_device(): landed = lax.all_to_all(pieces, 'elem', 0, 0)]
    gather x10 -> x0, local copies, waits for them, and re-layouts: 17.7 us -> none  [the longest x2 8.66 us: on_device(): nearby = pool[pool_index]]
    pallas_call x0 -> x4, Pallas kernels: none -> 14.8 us  [the longest x2 10.1 us: degree_step(): pl.pallas_call(body, name='degree_last' if last else 'degree', in_specs=[...]
    concatenate x4 -> x0, other arithmetic: 11.6 us -> none  [the longest x2 6.05 us: on_device(): jnp.concatenate([current[:, None], nearby], axis=1)]
    dot_general x3 -> x2, matrix products: 7.97 us -> 2.19 us  [gram(): lax.dot_general(left, right, (((0,), (0,)), ((), ())), preferred_element_...]
  transfers between devices with their start and end apart: 6 -> 5, of which waited for: 4 -> 4; matrix products, arithmetic and copies ran while one was open for 6% -> 0% of each run, Pallas kernels for 0% -> 2%
where the time goes in v1:
time: 85.7 us; the launch traced here: 85.3 us
  waiting for transfers between devices  32 us (37%)
  blocking collectives  19.6 us (23%)
  Pallas kernels  14.8 us (17%)
  starting transfers between devices  12.1 us (14%)
  local copies, waits for them, and re-layouts  3.23 us (4%)
  matrix products  2.19 us (3%)
    ppermute x5, waiting for transfers between devices, shifted(): lax.ppermute(block, axis, [((i - distance) % count, i) for i in range(cou...  32 us
    all_to_all x1, blocking collectives, on_device(): landed = lax.all_to_all(pieces, 'elem', 0, 0)  19.6 us
    ppermute x5, starting transfers between devices, shifted(): lax.ppermute(block, axis, [((i - distance) % count, i) for i in range(cou...  12.1 us
    pallas_call x2, Pallas kernels, degree_step(): pl.pallas_call(body, name='degree_last' if last else 'degree', in_specs=[...  10.1 us
    unnamed x11, local copies, waits for them, and re-layouts  3.23 us
    pallas_call x1, Pallas kernels, pack(): pl.pallas_call(body, name='pack', in_specs=[SM, SM, VM], out_specs=[VM, V...  2.6 us
    dot_general x2, matrix products, gram(): lax.dot_general(left, right, (((0,), (0,)), ((), ())), preferred_element_...  2.19 us
    pallas_call x1, Pallas kernels, tables(): pl.pallas_call(body, name='tables', in_specs=[SM], out_specs=[SM, SM], ou...  2.08 us
  transfers between devices with their start and end apart: 5, of which 4 were waited for; matrix products, arithmetic and copies ran while one was open for 0% of the time, Pallas kernels for 2%

profile of v1, /device:TPU:0, one launch (start us, length us, event | category | flops | bytes accessed | tf_op | source)
XLA Modules:
  0.0 85.3 jit_solution(10830764561690436972)
XLA Ops:
  0.6 1.4 %copy.7.near = s32[32,4]{1,0:T(8,128)} copy(s32[32,4]{0,1:T(4,128)} %param.9) | data formatting | bytes 1024 | tf_op args[4]
  2.0 2.6 %pack.1 = (bf16[16,64,256]{2,1,0:T(8,128)(2,1)}, bf16[16,64,256]{2,1,0:T(8,128)(2,1)}) custom-call(s32[32,4]{1,0:T(8,128)} %copy.7.near, s32[32]{0:T(128)} %sizes.5, bf16[32,64,256]{2,1,0:T(8,128)(2,1)} %previous.3), custom_call_target="tpu_custom_call" | custom-call | tf_op jit(solution)/shard_map/pack/pallas_call | solution.py:64
  4.6 0.5 collective-permute-start
  5.1 5.0 %collective-permute-start.1 = (bf16[16,64,256]{2,1,0:T(8,128)(2,1)}, bf16[16,64,256]{2,1,0:T(8,128)(2,1)S(1)}, u32[]{:S(2)}, u32[]{:S(2)}) collective-permute-start(bf16[16,64,256]{2,1,0:T(8,128)(2,1)} %get-tuple-element.12), channel_id=1, source_target_pairs={{2,0},{4,2},{6,4},{8,6},{10,8},{12,10},{14,12},{16,14},{18,16},{20... | collective-permute-start | bytes 1572872 | tf_op jit(solution)/shard_map/ppermute | solution.py:20
  10.1 2.1 %tables.1 = (s32[128]{0:T(128)}, s32[33]{0:T(128)}) custom-call(s32[32,4]{1,0:T(8,128)} %copy.7.near), custom_call_target="tpu_custom_call" | custom-call | tf_op jit(solution)/shard_map/tables/pallas_call | solution.py:105
  12.2 5.1 %collective-permute-done.from_prev = bf16[16,64,256]{2,1,0:T(8,128)(2,1)S(1)} collective-permute-done((bf16[16,64,256]{2,1,0:T(8,128)(2,1)}, bf16[16,64,256]{2,1,0:T(8,128)(2,1)S(1)}, u32[]{:S(2)}, u32[]{:S(2)}) %collective-permute-start) | collective-permute-done | bytes 524320 | tf_op jit(solution)/shard_map/ppermute | solution.py:20
  17.2 0.0 copy-start.3
  17.3 0.0 collective-permute-done.1.from_next
  17.3 0.0 copy-start.4
  17.3 0.8 copy-done.3
  18.0 0.2 copy-done.4
  18.2 5.2 %degree.1 = (bf16[32,64,256]{2,1,0:T(8,128)(2,1)}, bf16[16,64,256]{2,1,0:T(8,128)(2,1)}, bf16[16,64,256]{2,1,0:T(8,128)(2,1)}) custom-call(s32[128]{0:T(128)} %get-tuple-element.9.pool_index, s32[33]{0:T(128)} %get-tuple-element.10.orders, s32[32]{0:T(128)} %sizes.5, bf16[32,64,256]{2,1,0:T(8,128)(2,1)} %previous.3, bf16[32,64,256]{2,1,0:T(8,128)(2,1)} %previous.2, ...), custom_call_target="tpu_custom_call" | custom-call | tf_op jit(solution)/shard_map/degree/pallas_call | solution.py:151
  23.5 4.7 %collective-permute-start.2 = (bf16[16,64,256]{2,1,0:T(8,128)(2,1)}, bf16[16,64,256]{2,1,0:T(8,128)(2,1)S(1)}, u32[]{:S(2)}, u32[]{:S(2)}) collective-permute-start(bf16[16,64,256]{2,1,0:T(8,128)(2,1)} %get-tuple-element.14), channel_id=1, source_target_pairs={{30,0},{0,2},{2,4},{4,6},{6,8},{8,10},{10,12},{12,14},{14,16},{16,... | collective-permute-start | bytes 1572872 | tf_op jit(solution)/shard_map/ppermute | solution.py:20
  28.2 0.0 collective-permute-start.3
  28.2 6.9 %collective-permute-done.2.from_prev = bf16[16,64,256]{2,1,0:T(8,128)(2,1)S(1)} collective-permute-done((bf16[16,64,256]{2,1,0:T(8,128)(2,1)}, bf16[16,64,256]{2,1,0:T(8,128)(2,1)S(1)}, u32[]{:S(2)}, u32[]{:S(2)}) %collective-permute-start.2) | collective-permute-done | bytes 524320 | tf_op jit(solution)/shard_map/ppermute | solution.py:20
  35.1 0.0 copy-start.1
  35.1 0.1 collective-permute-done.3.from_next
  35.2 0.0 copy-start.2
  35.2 0.7 copy-done.1
  35.9 0.2 copy-done.2
  36.1 4.9 %degree_last.1 = bf16[32,64,256]{2,1,0:T(8,128)(2,1)} custom-call(s32[128]{0:T(128)} %get-tuple-element.9.pool_index, s32[33]{0:T(128)} %get-tuple-element.10.orders, s32[32]{0:T(128)} %sizes.5, bf16[32,64,256]{2,1,0:T(8,128)(2,1)} %get-tuple-element.13.current, bf16[32,64,256]{2,1,0:T(8,128)(2,1)} %previous.3, bf16[16,64,256]{2,1,0:T(8,128)(2,1)} %copy-done.1, ...), custom_call_target="tpu_custom_call" | custom-call | tf_op jit(solution)/shard_map/degree_last/pallas_call | solution.py:151
  41.0 0.0 copy-start
  41.0 1.9 %collective-permute-start.4 = (bf16[2048,256]{1,0:T(8,128)(2,1)}, bf16[2048,256]{1,0:T(8,128)(2,1)S(1)}, u32[]{:S(2)}, u32[]{:S(2)}) collective-permute-start(bf16[2048,256]{1,0:T(8,128)(2,1)} %bitcast.16), channel_id=1, source_target_pairs={{1,0},{0,1},{3,2},{2,3},{5,4},{4,5},{7,6},{6,7},{9,8},{8,9},{11,10... | collective-permute-start | bytes 3145736 | tf_op jit(solution)/shard_map/ppermute | solution.py:20
  42.9 19.9 %collective-permute-done.4 = bf16[2048,256]{1,0:T(8,128)(2,1)S(1)} collective-permute-done((bf16[2048,256]{1,0:T(8,128)(2,1)}, bf16[2048,256]{1,0:T(8,128)(2,1)S(1)}, u32[]{:S(2)}, u32[]{:S(2)}) %collective-permute-start.4) | collective-permute-done | bytes 1048608 | tf_op jit(solution)/shard_map/ppermute | solution.py:20
  62.8 1.7 %convolution_convert_fusion = bf16[256,256]{1,0:T(8,128)(2,1)S(1)} fusion(bf16[2048,256]{1,0:T(8,128)(2,1)S(1)} %collective-permute-done.4, bf16[2048,256]{1,0:T(8,128)(2,1)} %bitcast.17), kind=kOutput, calls=%fused_computation.2 | convolution fusion | flops 268500992 | bytes 2228224 | tf_op jit(solution)/shard_map/dot_general | solution.py:162
  64.5 0.0 copy-done
  64.5 0.5 select_bitcast_fusion.1
  65.1 19.6 %all_to_all.5 = bf16[16,32,256]{2,1,0:T(8,128)(2,1)S(1)} all-to-all(bf16[16,32,256]{2,1,0:T(8,128)(2,1)S(1)} %bitcast.18), channel_id=1, replica_groups=mesh['elem'=16,'band'=2] {'elem'}, dimensions={0} | all-to-all | bytes 524288 | tf_op jit(solution)/shard_map/all_to_all | solution.py:198
  84.7 0.6 broadcast_multiply_fusion
  (2 shorter events, 0.1 us)
Async XLA Ops:
  4.6 12.7 %collective-permute-start = (bf16[16,64,256]{2,1,0:T(8,128)(2,1)}, bf16[16,64,256]{2,1,0:T(8,128)(2,1)S(1)}, u32[]{:S(2)}, u32[]{:S(2)}) collective-permute-start(bf16[16,64,256]{2,1,0:T(8,128)(2,1)} %get-tuple-element.11), channel_id=1, source_target_pairs={{30,0},{0,2},{2,4},{4,6},{6,8},{8,10},{10,12},{12,14},{14,16},{16,... | collective-permute-start | bytes 1572872 | tf_op jit(solution)/shard_map/ppermute | solution.py:20
  5.1 12.2 %collective-permute-start.1 = (bf16[16,64,256]{2,1,0:T(8,128)(2,1)}, bf16[16,64,256]{2,1,0:T(8,128)(2,1)S(1)}, u32[]{:S(2)}, u32[]{:S(2)}) collective-permute-start(bf16[16,64,256]{2,1,0:T(8,128)(2,1)} %get-tuple-element.12), channel_id=1, source_target_pairs={{2,0},{4,2},{6,4},{8,6},{10,8},{12,10},{14,12},{16,14},{18,16},{20... | collective-permute-start | bytes 1572872 | tf_op jit(solution)/shard_map/ppermute | solution.py:20
  17.2 0.8 copy-start.3
  17.3 1.0 %copy-start.4 = (bf16[16,64,256]{2,1,0:T(8,128)(2,1)}, bf16[16,64,256]{2,1,0:T(8,128)(2,1)S(1)}, u32[]{:S(2)}) copy-start(bf16[16,64,256]{2,1,0:T(8,128)(2,1)S(1)} %collective-permute-done.1.from_next) | copy-start | bytes 1572868
  23.5 11.6 %collective-permute-start.2 = (bf16[16,64,256]{2,1,0:T(8,128)(2,1)}, bf16[16,64,256]{2,1,0:T(8,128)(2,1)S(1)}, u32[]{:S(2)}, u32[]{:S(2)}) collective-permute-start(bf16[16,64,256]{2,1,0:T(8,128)(2,1)} %get-tuple-element.14), channel_id=1, source_target_pairs={{30,0},{0,2},{2,4},{4,6},{6,8},{8,10},{10,12},{12,14},{14,16},{16,... | collective-permute-start | bytes 1572872 | tf_op jit(solution)/shard_map/ppermute | solution.py:20
  28.2 7.0 %collective-permute-start.3 = (bf16[16,64,256]{2,1,0:T(8,128)(2,1)}, bf16[16,64,256]{2,1,0:T(8,128)(2,1)S(1)}, u32[]{:S(2)}, u32[]{:S(2)}) collective-permute-start(bf16[16,64,256]{2,1,0:T(8,128)(2,1)} %get-tuple-element.15), channel_id=1, source_target_pairs={{2,0},{4,2},{6,4},{8,6},{10,8},{12,10},{14,12},{16,14},{18,16},{20... | collective-permute-start | bytes 1572872 | tf_op jit(solution)/shard_map/ppermute | solution.py:20
  35.1 0.8 copy-start.1
  35.2 0.9 %copy-start.2 = (bf16[16,64,256]{2,1,0:T(8,128)(2,1)}, bf16[16,64,256]{2,1,0:T(8,128)(2,1)S(1)}, u32[]{:S(2)}) copy-start(bf16[16,64,256]{2,1,0:T(8,128)(2,1)S(1)} %collective-permute-done.3.from_next) | copy-start | bytes 1572868
  41.0 23.5 %copy-start = (bf16[32,64,256]{2,1,0:T(8,128)(2,1)S(1)}, bf16[32,64,256]{2,1,0:T(8,128)(2,1)}, u32[]{:S(2)}) copy-start(bf16[32,64,256]{2,1,0:T(8,128)(2,1)} %degree_last.1) | copy-start | bytes 3145732
  41.0 21.8 %collective-permute-start.4 = (bf16[2048,256]{1,0:T(8,128)(2,1)}, bf16[2048,256]{1,0:T(8,128)(2,1)S(1)}, u32[]{:S(2)}, u32[]{:S(2)}) collective-permute-start(bf16[2048,256]{1,0:T(8,128)(2,1)} %bitcast.16), channel_id=1, source_target_pairs={{1,0},{0,1},{3,2},{2,3},{5,4},{4,5},{7,6},{6,7},{9,8},{8,9},{11,10... | collective-permute-start | bytes 3145736 | tf_op jit(solution)/shard_map/ppermute | solution.py:20

commit v2 on v1

--- a/solution.py
+++ b/solution.py
@@ -13,6 +13,7 @@
 
 VM = pl.BlockSpec(memory_space=pltpu.VMEM)
 SM = pl.BlockSpec(memory_space=pltpu.SMEM)
+GRANT = pltpu.CompilerParams(vmem_limit_bytes=16 * 1024 * 1024)
 
 
 def shifted(block, axis, distance):
@@ -36,8 +37,8 @@
     to_next = jnp.int32(0)
     to_prev = jnp.int32(0)
     for i in range(local_count):
-        lower = within(near[i, 1], base_next, local_count)
-        upper = within(near[i, 0], base_prev, local_count)
+        lower = within(near[1, i], base_next, local_count)
+        upper = within(near[0, i], base_prev, local_count)
         orders[jnp.where(lower, to_next, 2 * GY)] = i
         orders[jnp.where(upper, GY + to_prev, 2 * GY)] = i
         to_next = to_next + lower.astype(jnp.int32)
@@ -64,6 +65,7 @@
     return pl.pallas_call(
         body,
         name="pack",
+        compiler_params=GRANT,
         in_specs=[SM, SM, VM],
         out_specs=[VM, VM],
         out_shape=[halo, halo],
@@ -72,7 +74,7 @@
 
 
 def tables(near, count_elem):
-    local_count = near.shape[0]
+    local_count = near.shape[1]
 
     def body(near, pool_index, orders, slots, marks):
         bases = own_bases(local_count, count_elem)
@@ -81,10 +83,10 @@
         for j in range(2 * local_count):
             marks[j] = 0
         for i in range(local_count):
-            upper = within(near[i, 0], base_prev, local_count)
-            lower = within(near[i, 1], base_next, local_count)
-            marks[jnp.where(upper, near[i, 0] - base_prev, 2 * local_count)] = 1
-            marks[jnp.where(lower, local_count + near[i, 1] - base_next, 2 * local_count)] = 1
+            upper = within(near[0, i], base_prev, local_count)
+            lower = within(near[1, i], base_next, local_count)
+            marks[jnp.where(upper, near[0, i] - base_prev, 2 * local_count)] = 1
+            marks[jnp.where(lower, local_count + near[1, i] - base_next, 2 * local_count)] = 1
         from_prev = jnp.int32(local_count)
         from_next = jnp.int32(local_count + GY)
         for j in range(local_count):
@@ -93,18 +95,19 @@
             from_prev = from_prev + marks[j]
             from_next = from_next + marks[local_count + j]
         for i in range(local_count):
-            upper = within(near[i, 0], base_prev, local_count)
-            lower = within(near[i, 1], base_next, local_count)
-            far_prev = slots[jnp.where(upper, near[i, 0] - base_prev, 0)]
-            far_next = slots[jnp.where(lower, local_count + near[i, 1] - base_next, 0)]
-            pool_index[4 * i] = jnp.where(upper, far_prev, near[i, 0] - base)
-            pool_index[4 * i + 1] = jnp.where(lower, far_next, near[i, 1] - base)
-            pool_index[4 * i + 2] = near[i, 2] - base
-            pool_index[4 * i + 3] = near[i, 3] - base
+            upper = within(near[0, i], base_prev, local_count)
+            lower = within(near[1, i], base_next, local_count)
+            far_prev = slots[jnp.where(upper, near[0, i] - base_prev, 0)]
+            far_next = slots[jnp.where(lower, local_count + near[1, i] - base_next, 0)]
+            pool_index[4 * i] = jnp.where(upper, far_prev, near[0, i] - base)
+            pool_index[4 * i + 1] = jnp.where(lower, far_next, near[1, i] - base)
+            pool_index[4 * i + 2] = near[2, i] - base
+            pool_index[4 * i + 3] = near[3, i] - base
 
     return pl.pallas_call(
         body,
         name="tables",
+        compiler_params=GRANT,
         in_specs=[SM],
         out_specs=[SM, SM],
         out_shape=[
@@ -151,6 +154,7 @@
     return pl.pallas_call(
         body,
         name="degree_last" if last else "degree",
+        compiler_params=GRANT,
         in_specs=[SM, SM, SM] + [VM] * 5,
         out_specs=[VM] * len(outs),
         out_shape=outs,
@@ -158,10 +162,87 @@
     )(pool_index, orders, sizes, current, previous, from_prev, from_next, h_blocks)
 
 
-def gram(left, right):
-    return lax.dot_general(
-        left, right, (((0,), (0,)), ((), ())), preferred_element_type=jnp.float32
-    ).astype(jnp.bfloat16)
+def gram_pieces(blocks, count_elem, inner):
+    depth, width = blocks[0].shape
+    count_band = len(blocks)
+    outer = count_elem // inner
+    rows = count_band * width // count_elem
+
+    def body(*refs):
+        ins, outs, whole = refs[:count_band], refs[count_band:-1], refs[-1]
+        band = lax.axis_index("band")
+        place = lax.rem(lax.axis_index("elem"), inner)
+        for step in range(count_band):
+            source = lax.rem(band - step + count_band, count_band)
+            whole[pl.ds(pl.multiple_of(source * width, width), width), :] = lax.dot_general(
+                ins[step][...],
+                ins[0][...],
+                (((0,), (0,)), ((), ())),
+                preferred_element_type=jnp.float32,
+            )
+        for d in range(inner):
+            for o in range(outer):
+                start = pl.multiple_of((o * inner + (place ^ d)) * rows, rows)
+                outs[d][o] = whole[pl.ds(start, rows), :].astype(outs[d].dtype)
+
+    piece = (outer, rows, width)
+    return pl.pallas_call(
+        body,
+        name="gram",
+        compiler_params=GRANT,
+        in_specs=[VM] * count_band,
+        out_specs=[VM] * inner,
+        out_shape=[jax.ShapeDtypeStruct(piece, jnp.bfloat16 if d else jnp.float32) for d in range(inner)],
+        scratch_shapes=[pltpu.VMEM((count_band * width, width), jnp.float32)],
+    )(*blocks)
+
+
+def sum_pieces(own, landed, inner):
+    outer, rows, width = own.shape
+
+    def body(*refs):
+        ins, outs, whole = refs[: len(landed) + 1], refs[len(landed) + 1 : -1], refs[-1]
+        place = lax.div(lax.axis_index("elem"), inner)
+        total = ins[0][...]
+        for ref in ins[1:]:
+            total = total + ref[...].astype(jnp.float32)
+        whole[...] = total
+        for d in range(outer):
+            outs[d][...] = whole[place ^ d].astype(outs[d].dtype)
+
+    return pl.pallas_call(
+        body,
+        name="sum_inner",
+        compiler_params=GRANT,
+        in_specs=[VM] * (len(landed) + 1),
+        out_specs=[VM] * outer,
+        out_shape=[
+            jax.ShapeDtypeStruct((rows, width), jnp.bfloat16 if d else jnp.float32) for d in range(outer)
+        ],
+        scratch_shapes=[pltpu.VMEM((outer, rows, width), jnp.float32)],
+    )(own, *landed)
+
+
+def last_sum(own, landed, divisor):
+    def body(*refs):
+        total = refs[0][...]
+        for ref in refs[1:-1]:
+            total = total + ref[...].astype(jnp.float32)
+        refs[-1][...] = total / jnp.float32(divisor)
+
+    return pl.pallas_call(
+        body,
+        name="sum_outer",
+        compiler_params=GRANT,
+        in_specs=[VM] * (len(landed) + 1),
+        out_specs=VM,
+        out_shape=jax.ShapeDtypeStruct(own.shape, jnp.float32),
+    )(own, *landed)
+
+
+def paired(block, flip):
+    count = lax.axis_size("elem")
+    return lax.ppermute(block, "elem", [(i, i ^ flip) for i in range(count)])
 
 
 def on_device(y_current, y_previous, h_blocks, basis_sizes, neighbours):
@@ -169,6 +250,7 @@
     count_elem = lax.axis_size("elem")
     count_band = lax.axis_size("band")
     current, previous = y_current, y_previous
+    neighbours = neighbours.T
     to_next, to_prev = pack(current, basis_sizes, neighbours, count_elem)
     pool_index, orders = tables(neighbours, count_elem)
     for degree in range(DEGREES):
@@ -183,21 +265,14 @@
         if not last:
             to_next, to_prev = result[1:]
     flat = current.reshape(local_count * block, band_width)
-    band = lax.axis_index("band")
-    parts = [gram(flat, flat)]
-    for step in range(1, count_band):
-        parts.append(gram(shifted(flat, "band", step), flat))
-    if count_band == 2:
-        ordered = jnp.stack(
-            [jnp.where(band == 0, parts[0], parts[1]), jnp.where(band == 0, parts[1], parts[0])]
-        )
-    else:
-        ordered = jnp.stack(parts)[(band - jnp.arange(count_band)) % count_band]
-    rows = count_band * band_width // count_elem
-    pieces = ordered.reshape(count_elem, rows, band_width)
-    landed = lax.all_to_all(pieces, "elem", 0, 0)
-    summed = jnp.sum(landed.astype(jnp.float32), axis=0)
-    margin = summed / jnp.float32(local_count * count_elem * block)
+    blocks = [flat] + [shifted(flat, "band", step) for step in range(1, count_band)]
+    outer = 4
+    inner = count_elem // outer
+    pieces = gram_pieces(blocks, count_elem, inner)
+    landed = [paired(pieces[d], d) for d in range(1, inner)]
+    pieces = sum_pieces(pieces[0], landed, inner)
+    landed = [paired(pieces[d], d * inner) for d in range(1, outer)]
+    margin = last_sum(pieces[0], landed, local_count * count_elem * block)
     return (current, margin)
 
 

time: 85.7 us -> 81.3 us (0.949)
  blocking collectives: 19.6 us -> 0 us
  starting transfers between devices: 12.1 us -> 22.8 us
  waiting for transfers between devices: 32 us -> 40.8 us
  Pallas kernels: 14.8 us -> 9.57 us
  local copies, waits for them, and re-layouts: 3.23 us -> 7.07 us
  matrix products: 2.19 us -> 0 us
    all_to_all x1 -> x0, blocking collectives: 19.6 us -> none  [on_device(): landed = lax.all_to_all(pieces, 'elem', 0, 0)]
    ppermute x0 -> x6, starting transfers between devices: none -> 10.5 us  [paired(): return lax.ppermute(block, 'elem', [(i, i ^ flip) for i in range(count)])]
    ppermute x0 -> x6, waiting for transfers between devices: none -> 8.89 us  [paired(): return lax.ppermute(block, 'elem', [(i, i ^ flip) for i in range(count)])]
    pallas_call x4 -> x7, Pallas kernels: 14.8 us -> 9.57 us  [the longest x2 5.35 us: degree_step(): pl.pallas_call(body, name='degree_last' if last else 'degree', compiler_p...]
    unnamed x11 -> x18, local copies, waits for them, and re-layouts: 3.23 us -> 7.07 us
    dot_general x2 -> x0, matrix products: 2.19 us -> none  [gram(): lax.dot_general(left, right, (((0,), (0,)), ((), ())), preferred_element_...]
  transfers between devices with their start and end apart: 5 -> 11, of which waited for: 4 -> 8; matrix products, arithmetic and copies ran while one was open for 0% -> 0% of each run, Pallas kernels for 2% -> 2%
where the time goes in v2:
time: 81.3 us; the launch traced here: 81 us
  waiting for transfers between devices  40.8 us (50%)
  starting transfers between devices  22.8 us (28%)
  Pallas kernels  9.57 us (12%)
  local copies, waits for them, and re-layouts  7.07 us (9%)
    ppermute x5, waiting for transfers between devices, shifted(): lax.ppermute(block, axis, [((i - distance) % count, i) for i in range(cou...  31.9 us
    ppermute x5, starting transfers between devices, shifted(): lax.ppermute(block, axis, [((i - distance) % count, i) for i in range(cou...  12.3 us
    ppermute x6, starting transfers between devices, paired(): return lax.ppermute(block, 'elem', [(i, i ^ flip) for i in range(count)])  10.5 us
    ppermute x6, waiting for transfers between devices, paired(): return lax.ppermute(block, 'elem', [(i, i ^ flip) for i in range(count)])  8.89 us
    unnamed x18, local copies, waits for them, and re-layouts  7.07 us
    pallas_call x2, Pallas kernels, degree_step(): pl.pallas_call(body, name='degree_last' if last else 'degree', compiler_p...  5.35 us
    pallas_call x1, Pallas kernels, tables(): pl.pallas_call(body, name='tables', compiler_params=GRANT, in_specs=[SM],...  1.8 us
  transfers between devices with their start and end apart: 11, of which 8 were waited for; matrix products, arithmetic and copies ran while one was open for 0% of the time, Pallas kernels for 2%

profile of v2, /device:TPU:0, one launch (start us, length us, event | category | flops | bytes accessed | tf_op | source)
XLA Modules:
  0.0 81.0 jit_solution(11917384014711468516)
XLA Ops:
  0.6 0.0 copy-start
  0.6 1.2 %copy-done = bf16[32,64,256]{2,1,0:T(8,128)(2,1)S(1)} copy-done((bf16[32,64,256]{2,1,0:T(8,128)(2,1)S(1)}, bf16[32,64,256]{2,1,0:T(8,128)(2,1)}, u32[]{:S(2)}) %copy-start) | copy-done | bytes 1048600
  1.9 0.0 copy-start.6
  1.9 0.7 copy-done.6
  2.5 0.0 copy-start.7
  2.5 0.7 copy-done.7
  3.2 0.0 copy-start.1
  3.2 1.0 %pack.1 = (bf16[16,64,256]{2,1,0:T(8,128)(2,1)S(1)}, bf16[16,64,256]{2,1,0:T(8,128)(2,1)S(1)}) custom-call(s32[4,32]{1,0:T(4,128)S(1)} %bitcast.4, s32[32]{0:T(128)S(1)} %copy-done.7, bf16[32,64,256]{2,1,0:T(8,128)(2,1)S(1)} %copy-done), custom_call_target="tpu_custom_call" | custom-call | tf_op jit(solution)/shard_map/pack/pallas_call | solution.py:65
  4.2 0.5 collective-permute-start
  4.7 5.0 %collective-permute-start.1 = (bf16[16,64,256]{2,1,0:T(8,128)(2,1)S(1)}, bf16[16,64,256]{2,1,0:T(8,128)(2,1)S(1)}, u32[]{:S(2)}, u32[]{:S(2)}) collective-permute-start(bf16[16,64,256]{2,1,0:T(8,128)(2,1)S(1)} %get-tuple-element.20), channel_id=1, source_target_pairs={{2,0},{4,2},{6,4},{8,6},{10,8},{12,10},{14,12},{16,14},{18,16},{20... | collective-permute-start | bytes 1572872 | tf_op jit(solution)/shard_map/ppermute | solution.py:21
  9.8 1.8 %tables.1 = (s32[128]{0:T(128)S(1)}, s32[33]{0:T(128)S(1)}) custom-call(s32[4,32]{1,0:T(4,128)S(1)} %bitcast.5), custom_call_target="tpu_custom_call" | custom-call | tf_op jit(solution)/shard_map/tables/pallas_call | solution.py:107
  11.6 5.1 %collective-permute-done.from_prev = bf16[16,64,256]{2,1,0:T(8,128)(2,1)S(1)} collective-permute-done((bf16[16,64,256]{2,1,0:T(8,128)(2,1)S(1)}, bf16[16,64,256]{2,1,0:T(8,128)(2,1)S(1)}, u32[]{:S(2)}, u32[]{:S(2)}) %collective-permute-start) | collective-permute-done | bytes 524320 | tf_op jit(solution)/shard_map/ppermute | solution.py:21
  16.7 0.0 collective-permute-done.1.from_next
  16.7 0.0 copy-done.1
  16.7 0.0 copy-start.2
  16.7 1.4 %copy-done.2 = bf16[32,64,320]{2,1,0:T(8,128)(2,1)S(1)} copy-done((bf16[32,64,320]{2,1,0:T(8,128)(2,1)S(1)}, bf16[32,64,320]{2,1,0:T(8,128)(2,1)}, u32[]{:S(2)}) %copy-start.2) | copy-done | bytes 1310744
  18.1 0.0 copy-start.5
  18.1 1.2 %copy-done.5 = bf16[32,64,256]{2,1,0:T(8,128)(2,1)S(1)} copy-done((bf16[32,64,256]{2,1,0:T(8,128)(2,1)S(1)}, bf16[32,64,256]{2,1,0:T(8,128)(2,1)}, u32[]{:S(2)}) %copy-start.5) | copy-done | bytes 1048600
  19.3 0.0 copy-start.8
  19.3 0.7 copy-done.8
  20.0 0.0 copy-start.3
  20.0 2.2 %degree.1 = (bf16[32,64,256]{2,1,0:T(8,128)(2,1)S(1)}, bf16[16,64,256]{2,1,0:T(8,128)(2,1)S(1)}, bf16[16,64,256]{2,1,0:T(8,128)(2,1)S(1)}) custom-call(s32[128]{0:T(128)S(1)} %get-tuple-element.17.pool_index, s32[33]{0:T(128)S(1)} %get-tuple-element.18.orders, s32[32]{0:T(128)S(1)} %copy-done.8, bf16[32,64,256]{2,1,0:T(8,128)(2,1)S(1)} %copy-done.1, ...), custom_call_target="tpu_custom_call" | custom-call | tf_op jit(solution)/shard_map/degree/pallas_call | solution.py:154
  22.2 4.9 %collective-permute-start.2 = (bf16[16,64,256]{2,1,0:T(8,128)(2,1)S(1)}, bf16[16,64,256]{2,1,0:T(8,128)(2,1)S(1)}, u32[]{:S(2)}, u32[]{:S(2)}) collective-permute-start(bf16[16,64,256]{2,1,0:T(8,128)(2,1)S(1)} %get-tuple-element.22), channel_id=1, source_target_pairs={{30,0},{0,2},{2,4},{4,6},{6,8},{8,10},{10,12},{12,14},{14,16},{16,... | collective-permute-start | bytes 1572872 | tf_op jit(solution)/shard_map/ppermute | solution.py:21
  27.1 0.0 collective-permute-start.3
  27.2 6.6 %collective-permute-done.2.from_prev = bf16[16,64,256]{2,1,0:T(8,128)(2,1)S(1)} collective-permute-done((bf16[16,64,256]{2,1,0:T(8,128)(2,1)S(1)}, bf16[16,64,256]{2,1,0:T(8,128)(2,1)S(1)}, u32[]{:S(2)}, u32[]{:S(2)}) %collective-permute-start.2) | collective-permute-done | bytes 524320 | tf_op jit(solution)/shard_map/ppermute | solution.py:21
  33.7 0.1 collective-permute-done.3.from_next
  33.9 0.0 copy-done.3
  33.9 3.1 %degree_last.1 = bf16[32,64,256]{2,1,0:T(8,128)(2,1)} custom-call(s32[128]{0:T(128)S(1)} %get-tuple-element.17.pool_index, s32[33]{0:T(128)S(1)} %get-tuple-element.18.orders, s32[32]{0:T(128)S(1)} %copy-done.8, bf16[32,64,256]{2,1,0:T(8,128)(2,1)S(1)} %get-tuple-element.21.current, bf16[32,64,256]{2,1,0:T(8,128)(2,1)S(1)} %copy-done.1, ...), custom_call_target="tpu_custom_call" | custom-call | tf_op jit(solution)/shard_map/degree_last/pallas_call | solution.py:154
  37.0 1.8 %collective-permute-start.4 = (bf16[2048,256]{1,0:T(8,128)(2,1)}, bf16[2048,256]{1,0:T(8,128)(2,1)S(1)}, u32[]{:S(2)}, u32[]{:S(2)}) collective-permute-start(bf16[2048,256]{1,0:T(8,128)(2,1)} %bitcast.2), channel_id=1, source_target_pairs={{1,0},{0,1},{3,2},{2,3},{5,4},{4,5},{7,6},{6,7},{9,8},{8,9},{11,10... | collective-permute-start | bytes 3145736 | tf_op jit(solution)/shard_map/ppermute | solution.py:21
  38.7 20.1 %collective-permute-done.4.refs_1_ = bf16[2048,256]{1,0:T(8,128)(2,1)S(1)} collective-permute-done((bf16[2048,256]{1,0:T(8,128)(2,1)}, bf16[2048,256]{1,0:T(8,128)(2,1)S(1)}, u32[]{:S(2)}, u32[]{:S(2)}) %collective-permute-start.4) | collective-permute-done | bytes 1048608 | tf_op jit(solution)/shard_map/ppermute | solution.py:21
  58.9 0.0 copy-start.4
  58.9 1.2 %copy-done.4 = bf16[32,64,256]{2,1,0:T(8,128)(2,1)S(1)} copy-done((bf16[32,64,256]{2,1,0:T(8,128)(2,1)S(1)}, bf16[32,64,256]{2,1,0:T(8,128)(2,1)}, u32[]{:S(2)}) %copy-start.4) | copy-done | bytes 1048600
  60.1 0.8 gram.1
  60.9 4.3 %collective-permute-start.5 = (bf16[4,32,256]{2,1,0:T(8,128)(2,1)S(1)}, bf16[4,32,256]{2,1,0:T(8,128)(2,1)S(1)}, u32[]{:S(2)}, u32[]{:S(2)}) collective-permute-start(bf16[4,32,256]{2,1,0:T(8,128)(2,1)S(1)} %get-tuple-element.25), channel_id=1, source_target_pairs={{0,2},{2,0},{4,6},{6,4},{8,10},{10,8},{12,14},{14,12},{16,18},{18,... | collective-permute-start | bytes 196616 | tf_op jit(solution)/shard_map/ppermute | solution.py:245
  65.1 1.8 %collective-permute-start.6 = (bf16[4,32,256]{2,1,0:T(8,128)(2,1)S(1)}, bf16[4,32,256]{2,1,0:T(8,128)(2,1)S(1)}, u32[]{:S(2)}, u32[]{:S(2)}) collective-permute-start(bf16[4,32,256]{2,1,0:T(8,128)(2,1)S(1)} %get-tuple-element.26), channel_id=1, source_target_pairs={{0,4},{2,6},{4,0},{6,2},{8,12},{10,14},{12,8},{14,10},{16,20},{18,... | collective-permute-start | bytes 196616 | tf_op jit(solution)/shard_map/ppermute | solution.py:245
  66.9 0.0 collective-permute-start.7
  67.0 0.0 collective-permute-done.5.refs_1_
  67.0 2.6 %collective-permute-done.6.refs_2_ = bf16[4,32,256]{2,1,0:T(8,128)(2,1)S(1)} collective-permute-done((bf16[4,32,256]{2,1,0:T(8,128)(2,1)S(1)}, bf16[4,32,256]{2,1,0:T(8,128)(2,1)S(1)}, u32[]{:S(2)}, u32[]{:S(2)}) %collective-permute-start.6) | collective-permute-done | bytes 65568 | tf_op jit(solution)/shard_map/ppermute | solution.py:245
  69.6 1.4 %collective-permute-done.7.refs_3_ = bf16[4,32,256]{2,1,0:T(8,128)(2,1)S(1)} collective-permute-done((bf16[4,32,256]{2,1,0:T(8,128)(2,1)S(1)}, bf16[4,32,256]{2,1,0:T(8,128)(2,1)S(1)}, u32[]{:S(2)}, u32[]{:S(2)}) %collective-permute-start.7) | collective-permute-done | bytes 65568 | tf_op jit(solution)/shard_map/ppermute | solution.py:245
  71.0 1.6 %collective-permute-start.8 = (bf16[32,256]{1,0:T(8,128)(2,1)S(1)}, bf16[32,256]{1,0:T(8,128)(2,1)S(1)}, u32[]{:S(2)}, u32[]{:S(2)}) collective-permute-start(bf16[32,256]{1,0:T(8,128)(2,1)S(1)} %get-tuple-element.29), channel_id=1, source_target_pairs={{0,8},{2,10},{4,12},{6,14},{8,0},{10,2},{12,4},{14,6},{16,24},{18,... | collective-permute-start | bytes 49160 | tf_op jit(solution)/shard_map/ppermute | solution.py:245
  72.7 2.1 %collective-permute-start.9 = (bf16[32,256]{1,0:T(8,128)(2,1)S(1)}, bf16[32,256]{1,0:T(8,128)(2,1)S(1)}, u32[]{:S(2)}, u32[]{:S(2)}) collective-permute-start(bf16[32,256]{1,0:T(8,128)(2,1)S(1)} %get-tuple-element.30), channel_id=1, source_target_pairs={{0,16},{2,18},{4,20},{6,22},{8,24},{10,26},{12,28},{14,30},{16,0},... | collective-permute-start | bytes 49160 | tf_op jit(solution)/shard_map/ppermute | solution.py:245
  74.8 0.7 collective-permute-start.10
  75.5 0.0 collective-permute-done.8.refs_1_
  75.5 1.9 %collective-permute-done.9.refs_2_ = bf16[32,256]{1,0:T(8,128)(2,1)S(1)} collective-permute-done((bf16[32,256]{1,0:T(8,128)(2,1)S(1)}, bf16[32,256]{1,0:T(8,128)(2,1)S(1)}, u32[]{:S(2)}, u32[]{:S(2)}) %collective-permute-start.9) | collective-permute-done | bytes 16416 | tf_op jit(solution)/shard_map/ppermute | solution.py:245
  77.4 3.0 %collective-permute-done.10.refs_3_ = bf16[32,256]{1,0:T(8,128)(2,1)S(1)} collective-permute-done((bf16[32,256]{1,0:T(8,128)(2,1)S(1)}, bf16[32,256]{1,0:T(8,128)(2,1)S(1)}, u32[]{:S(2)}, u32[]{:S(2)}) %collective-permute-start.10) | collective-permute-done | bytes 16416 | tf_op jit(solution)/shard_map/ppermute | solution.py:245
  80.3 0.6 sum_outer.1
  (1 shorter events, 0.0 us)
Async XLA Ops:
  0.6 1.2 %copy-start = (bf16[32,64,256]{2,1,0:T(8,128)(2,1)S(1)}, bf16[32,64,256]{2,1,0:T(8,128)(2,1)}, u32[]{:S(2)}) copy-start(bf16[32,64,256]{2,1,0:T(8,128)(2,1)} %previous.3) | copy-start | bytes 3145732
  1.9 0.7 copy-start.6
  2.5 0.7 copy-start.7
  3.2 13.5 %copy-start.1 = (bf16[32,64,256]{2,1,0:T(8,128)(2,1)S(1)}, bf16[32,64,256]{2,1,0:T(8,128)(2,1)}, u32[]{:S(2)}) copy-start(bf16[32,64,256]{2,1,0:T(8,128)(2,1)} %previous.3) | copy-start | bytes 3145732
  4.2 12.5 %collective-permute-start = (bf16[16,64,256]{2,1,0:T(8,128)(2,1)S(1)}, bf16[16,64,256]{2,1,0:T(8,128)(2,1)S(1)}, u32[]{:S(2)}, u32[]{:S(2)}) collective-permute-start(bf16[16,64,256]{2,1,0:T(8,128)(2,1)S(1)} %get-tuple-element.19), channel_id=1, source_target_pairs={{30,0},{0,2},{2,4},{4,6},{6,8},{8,10},{10,12},{12,14},{14,16},{16,... | collective-permute-start | bytes 1572872 | tf_op jit(solution)/shard_map/ppermute | solution.py:21
  4.7 11.9 %collective-permute-start.1 = (bf16[16,64,256]{2,1,0:T(8,128)(2,1)S(1)}, bf16[16,64,256]{2,1,0:T(8,128)(2,1)S(1)}, u32[]{:S(2)}, u32[]{:S(2)}) collective-permute-start(bf16[16,64,256]{2,1,0:T(8,128)(2,1)S(1)} %get-tuple-element.20), channel_id=1, source_target_pairs={{2,0},{4,2},{6,4},{8,6},{10,8},{12,10},{14,12},{16,14},{18,16},{20... | collective-permute-start | bytes 1572872 | tf_op jit(solution)/shard_map/ppermute | solution.py:21
  16.7 1.4 %copy-start.2 = (bf16[32,64,320]{2,1,0:T(8,128)(2,1)S(1)}, bf16[32,64,320]{2,1,0:T(8,128)(2,1)}, u32[]{:S(2)}) copy-start(bf16[32,64,320]{2,1,0:T(8,128)(2,1)} %h_blocks.3) | copy-start | bytes 3932164
  18.1 1.2 %copy-start.5 = (bf16[32,64,256]{2,1,0:T(8,128)(2,1)S(1)}, bf16[32,64,256]{2,1,0:T(8,128)(2,1)}, u32[]{:S(2)}) copy-start(bf16[32,64,256]{2,1,0:T(8,128)(2,1)} %previous.2) | copy-start | bytes 3145732
  19.3 0.7 copy-start.8
  20.0 13.9 %copy-start.3 = (bf16[32,64,320]{2,1,0:T(8,128)(2,1)S(1)}, bf16[32,64,320]{2,1,0:T(8,128)(2,1)}, u32[]{:S(2)}) copy-start(bf16[32,64,320]{2,1,0:T(8,128)(2,1)} %h_blocks.3) | copy-start | bytes 3932164
  22.2 11.5 %collective-permute-start.2 = (bf16[16,64,256]{2,1,0:T(8,128)(2,1)S(1)}, bf16[16,64,256]{2,1,0:T(8,128)(2,1)S(1)}, u32[]{:S(2)}, u32[]{:S(2)}) collective-permute-start(bf16[16,64,256]{2,1,0:T(8,128)(2,1)S(1)} %get-tuple-element.22), channel_id=1, source_target_pairs={{30,0},{0,2},{2,4},{4,6},{6,8},{8,10},{10,12},{12,14},{14,16},{16,... | collective-permute-start | bytes 1572872 | tf_op jit(solution)/shard_map/ppermute | solution.py:21
  27.1 6.7 %collective-permute-start.3 = (bf16[16,64,256]{2,1,0:T(8,128)(2,1)S(1)}, bf16[16,64,256]{2,1,0:T(8,128)(2,1)S(1)}, u32[]{:S(2)}, u32[]{:S(2)}) collective-permute-start(bf16[16,64,256]{2,1,0:T(8,128)(2,1)S(1)} %get-tuple-element.23), channel_id=1, source_target_pairs={{2,0},{4,2},{6,4},{8,6},{10,8},{12,10},{14,12},{16,14},{18,16},{20... | collective-permute-start | bytes 1572872 | tf_op jit(solution)/shard_map/ppermute | solution.py:21
  37.0 21.9 %collective-permute-start.4 = (bf16[2048,256]{1,0:T(8,128)(2,1)}, bf16[2048,256]{1,0:T(8,128)(2,1)S(1)}, u32[]{:S(2)}, u32[]{:S(2)}) collective-permute-start(bf16[2048,256]{1,0:T(8,128)(2,1)} %bitcast.2), channel_id=1, source_target_pairs={{1,0},{0,1},{3,2},{2,3},{5,4},{4,5},{7,6},{6,7},{9,8},{8,9},{11,10... | collective-permute-start | bytes 3145736 | tf_op jit(solution)/shard_map/ppermute | solution.py:21
  58.9 1.2 %copy-start.4 = (bf16[32,64,256]{2,1,0:T(8,128)(2,1)S(1)}, bf16[32,64,256]{2,1,0:T(8,128)(2,1)}, u32[]{:S(2)}) copy-start(bf16[32,64,256]{2,1,0:T(8,128)(2,1)} %degree_last.1) | copy-start | bytes 3145732
  60.9 6.1 %collective-permute-start.5 = (bf16[4,32,256]{2,1,0:T(8,128)(2,1)S(1)}, bf16[4,32,256]{2,1,0:T(8,128)(2,1)S(1)}, u32[]{:S(2)}, u32[]{:S(2)}) collective-permute-start(bf16[4,32,256]{2,1,0:T(8,128)(2,1)S(1)} %get-tuple-element.25), channel_id=1, source_target_pairs={{0,2},{2,0},{4,6},{6,4},{8,10},{10,8},{12,14},{14,12},{16,18},{18,... | collective-permute-start | bytes 196616 | tf_op jit(solution)/shard_map/ppermute | solution.py:245
  65.1 4.5 %collective-permute-start.6 = (bf16[4,32,256]{2,1,0:T(8,128)(2,1)S(1)}, bf16[4,32,256]{2,1,0:T(8,128)(2,1)S(1)}, u32[]{:S(2)}, u32[]{:S(2)}) collective-permute-start(bf16[4,32,256]{2,1,0:T(8,128)(2,1)S(1)} %get-tuple-element.26), channel_id=1, source_target_pairs={{0,4},{2,6},{4,0},{6,2},{8,12},{10,14},{12,8},{14,10},{16,20},{18,... | collective-permute-start | bytes 196616 | tf_op jit(solution)/shard_map/ppermute | solution.py:245
  66.9 4.1 %collective-permute-start.7 = (bf16[4,32,256]{2,1,0:T(8,128)(2,1)S(1)}, bf16[4,32,256]{2,1,0:T(8,128)(2,1)S(1)}, u32[]{:S(2)}, u32[]{:S(2)}) collective-permute-start(bf16[4,32,256]{2,1,0:T(8,128)(2,1)S(1)} %get-tuple-element.27), channel_id=1, source_target_pairs={{0,6},{2,4},{4,2},{6,0},{8,14},{10,12},{12,10},{14,8},{16,22},{18,... | collective-permute-start | bytes 196616 | tf_op jit(solution)/shard_map/ppermute | solution.py:245
  71.0 4.5 %collective-permute-start.8 = (bf16[32,256]{1,0:T(8,128)(2,1)S(1)}, bf16[32,256]{1,0:T(8,128)(2,1)S(1)}, u32[]{:S(2)}, u32[]{:S(2)}) collective-permute-start(bf16[32,256]{1,0:T(8,128)(2,1)S(1)} %get-tuple-element.29), channel_id=1, source_target_pairs={{0,8},{2,10},{4,12},{6,14},{8,0},{10,2},{12,4},{14,6},{16,24},{18,... | collective-permute-start | bytes 49160 | tf_op jit(solution)/shard_map/ppermute | solution.py:245
  72.7 4.7 %collective-permute-start.9 = (bf16[32,256]{1,0:T(8,128)(2,1)S(1)}, bf16[32,256]{1,0:T(8,128)(2,1)S(1)}, u32[]{:S(2)}, u32[]{:S(2)}) collective-permute-start(bf16[32,256]{1,0:T(8,128)(2,1)S(1)} %get-tuple-element.30), channel_id=1, source_target_pairs={{0,16},{2,18},{4,20},{6,22},{8,24},{10,26},{12,28},{14,30},{16,0},... | collective-permute-start | bytes 49160 | tf_op jit(solution)/shard_map/ppermute | solution.py:245
  74.8 5.5 %collective-permute-start.10 = (bf16[32,256]{1,0:T(8,128)(2,1)S(1)}, bf16[32,256]{1,0:T(8,128)(2,1)S(1)}, u32[]{:S(2)}, u32[]{:S(2)}) collective-permute-start(bf16[32,256]{1,0:T(8,128)(2,1)S(1)} %get-tuple-element.31), channel_id=1, source_target_pairs={{0,24},{2,26},{4,28},{6,30},{8,16},{10,18},{12,20},{14,22},{16,8},... | collective-permute-start | bytes 49160 | tf_op jit(solution)/shard_map/ppermute | solution.py:245

commit v3 on v2

--- a/solution.py
+++ b/solution.py
@@ -73,10 +73,14 @@
     )(near, sizes, values)
 
 
-def tables(near, count_elem):
+def tables(near, sizes, h_blocks, previous, count_elem):
     local_count = near.shape[1]
 
-    def body(near, pool_index, orders, slots, marks):
+    def body(near, sizes, h_blocks, previous, pool_index, orders, extents, h_held, held, slots, marks):
+        h_held[...] = h_blocks[...]
+        held[...] = previous[...]
+        for i in range(local_count):
+            extents[i] = sizes[i]
         bases = own_bases(local_count, count_elem)
         base_prev, base, base_next = bases
         send_lists(near, orders, local_count, bases)
@@ -108,17 +112,20 @@
         body,
         name="tables",
         compiler_params=GRANT,
-        in_specs=[SM],
-        out_specs=[SM, SM],
+        in_specs=[SM, SM, VM, VM],
+        out_specs=[SM, SM, SM, VM, VM],
         out_shape=[
             jax.ShapeDtypeStruct((4 * local_count,), jnp.int32),
             jax.ShapeDtypeStruct((2 * GY + 1,), jnp.int32),
+            jax.ShapeDtypeStruct(sizes.shape, jnp.int32),
+            jax.ShapeDtypeStruct(h_blocks.shape, h_blocks.dtype),
+            jax.ShapeDtypeStruct(previous.shape, previous.dtype),
         ],
         scratch_shapes=[
             pltpu.SMEM((2 * local_count,), jnp.int32),
             pltpu.SMEM((2 * local_count + 1,), jnp.int32),
         ],
-    )(near)
+    )(near, sizes, h_blocks, previous)
 
 
 def degree_step(pool_index, orders, sizes, current, previous, from_prev, from_next, h_blocks, last):
@@ -142,7 +149,9 @@
                 applied - center_value * own.astype(jnp.float32)
             ) - previous[i].astype(jnp.float32)
             following[i] = jnp.where(rows < sizes[i], value, 0.0).astype(jnp.bfloat16)
-        if not last:
+        if last:
+            rest[0][...] = following[...]
+        else:
             to_next, to_prev = rest[:2]
             for s in range(GY):
                 to_next[s] = following[orders[s]]
@@ -150,7 +159,7 @@
 
     whole = jax.ShapeDtypeStruct(current.shape, jnp.bfloat16)
     halo = jax.ShapeDtypeStruct((GY, block, width), jnp.bfloat16)
-    outs = [whole] if last else [whole, halo, halo]
+    outs = [whole, whole] if last else [whole, halo, halo]
     return pl.pallas_call(
         body,
         name="degree_last" if last else "degree",
@@ -162,82 +171,79 @@
     )(pool_index, orders, sizes, current, previous, from_prev, from_next, h_blocks)
 
 
-def gram_pieces(blocks, count_elem, inner):
+def split_rows(whole, keep, send, bit):
+    for g in range(keep.shape[0]):
+        keep[g] = whole[2 * g + bit].astype(keep.dtype)
+        send[g] = whole[2 * g + 1 - bit].astype(send.dtype)
+
+
+def split_shapes(groups, rows, width):
+    piece = (groups // 2, rows, width)
+    return [jax.ShapeDtypeStruct(piece, jnp.float32), jax.ShapeDtypeStruct(piece, jnp.bfloat16)]
+
+
+def gram_pieces(blocks, count_elem):
     depth, width = blocks[0].shape
     count_band = len(blocks)
-    outer = count_elem // inner
     rows = count_band * width // count_elem
+    per_band = width // rows
 
     def body(*refs):
-        ins, outs, whole = refs[:count_band], refs[count_band:-1], refs[-1]
+        ins, keep, send, whole = refs[:count_band], *refs[count_band:]
         band = lax.axis_index("band")
-        place = lax.rem(lax.axis_index("elem"), inner)
         for step in range(count_band):
             source = lax.rem(band - step + count_band, count_band)
-            whole[pl.ds(pl.multiple_of(source * width, width), width), :] = lax.dot_general(
+            product = lax.dot_general(
                 ins[step][...],
                 ins[0][...],
                 (((0,), (0,)), ((), ())),
                 preferred_element_type=jnp.float32,
             )
-        for d in range(inner):
-            for o in range(outer):
-                start = pl.multiple_of((o * inner + (place ^ d)) * rows, rows)
-                outs[d][o] = whole[pl.ds(start, rows), :].astype(outs[d].dtype)
-
-    piece = (outer, rows, width)
+            for r in range(per_band):
+                whole[source * per_band + r] = product[r * rows : (r + 1) * rows]
+        split_rows(whole, keep, send, lax.rem(lax.axis_index("elem"), 2))
+
     return pl.pallas_call(
         body,
         name="gram",
         compiler_params=GRANT,
         in_specs=[VM] * count_band,
-        out_specs=[VM] * inner,
-        out_shape=[jax.ShapeDtypeStruct(piece, jnp.bfloat16 if d else jnp.float32) for d in range(inner)],
-        scratch_shapes=[pltpu.VMEM((count_band * width, width), jnp.float32)],
+        out_specs=[VM, VM],
+        out_shape=split_shapes(count_elem, rows, width),
+        scratch_shapes=[pltpu.VMEM((count_elem, rows, width), jnp.float32)],
     )(*blocks)
 
 
-def sum_pieces(own, landed, inner):
-    outer, rows, width = own.shape
-
-    def body(*refs):
-        ins, outs, whole = refs[: len(landed) + 1], refs[len(landed) + 1 : -1], refs[-1]
-        place = lax.div(lax.axis_index("elem"), inner)
-        total = ins[0][...]
-        for ref in ins[1:]:
-            total = total + ref[...].astype(jnp.float32)
-        whole[...] = total
-        for d in range(outer):
-            outs[d][...] = whole[place ^ d].astype(outs[d].dtype)
-
-    return pl.pallas_call(
-        body,
-        name="sum_inner",
-        compiler_params=GRANT,
-        in_specs=[VM] * (len(landed) + 1),
-        out_specs=[VM] * outer,
-        out_shape=[
-            jax.ShapeDtypeStruct((rows, width), jnp.bfloat16 if d else jnp.float32) for d in range(outer)
-        ],
-        scratch_shapes=[pltpu.VMEM((outer, rows, width), jnp.float32)],
-    )(own, *landed)
-
-
-def last_sum(own, landed, divisor):
-    def body(*refs):
-        total = refs[0][...]
-        for ref in refs[1:-1]:
-            total = total + ref[...].astype(jnp.float32)
-        refs[-1][...] = total / jnp.float32(divisor)
-
-    return pl.pallas_call(
-        body,
-        name="sum_outer",
-        compiler_params=GRANT,
-        in_specs=[VM] * (len(landed) + 1),
+def halve(kept, landed, flip):
+    groups, rows, width = kept.shape
+
+    def body(kept, landed, keep, send, whole):
+        whole[...] = kept[...] + landed[...].astype(jnp.float32)
+        split_rows(whole, keep, send, lax.rem(lax.div(lax.axis_index("elem"), flip), 2))
+
+    return pl.pallas_call(
+        body,
+        name="halve",
+        compiler_params=GRANT,
+        in_specs=[VM, VM],
+        out_specs=[VM, VM],
+        out_shape=split_shapes(groups, rows, width),
+        scratch_shapes=[pltpu.VMEM((groups, rows, width), jnp.float32)],
+    )(kept, landed)
+
+
+def last_sum(kept, landed, divisor):
+    def body(kept, landed, out):
+        out[...] = (kept[0] + landed[0].astype(jnp.float32)) / jnp.float32(divisor)
+
+    return pl.pallas_call(
+        body,
+        name="last_sum",
+        compiler_params=GRANT,
+        in_specs=[VM, VM],
         out_specs=VM,
-        out_shape=jax.ShapeDtypeStruct(own.shape, jnp.float32),
-    )(own, *landed)
+        out_shape=jax.ShapeDtypeStruct(kept.shape[1:], jnp.float32),
+    )(kept, landed)
 
 
 def paired(block, flip):
@@ -252,27 +258,31 @@
     current, previous = y_current, y_previous
     neighbours = neighbours.T
     to_next, to_prev = pack(current, basis_sizes, neighbours, count_elem)
-    pool_index, orders = tables(neighbours, count_elem)
+    pool_index, orders, sizes, h_blocks, previous = tables(
+        neighbours, basis_sizes, h_blocks, previous, count_elem
+    )
     for degree in range(DEGREES):
         from_prev = shifted(to_next, "elem", 1)
         from_next = shifted(to_prev, "elem", -1)
         last = degree == DEGREES - 1
         result = degree_step(
-            pool_index, orders, basis_sizes, current, previous, from_prev, from_next, h_blocks, last
+            pool_index, orders, sizes, current, previous, from_prev, from_next, h_blocks, last
         )
         previous = current
         current = result[0]
         if not last:
             to_next, to_prev = result[1:]
-    flat = current.reshape(local_count * block, band_width)
+    flat = result[1]
+    flat = flat.reshape(local_count * block, band_width)
     blocks = [flat] + [shifted(flat, "band", step) for step in range(1, count_band)]
-    outer = 4
-    inner = count_elem // outer
-    pieces = gram_pieces(blocks, count_elem, inner)
-    landed = [paired(pieces[d], d) for d in range(1, inner)]
-    pieces = sum_pieces(pieces[0], landed, inner)
-    landed = [paired(pieces[d], d * inner) for d in range(1, outer)]
-    margin = last_sum(pieces[0], landed, local_count * count_elem * block)
+    keep, send = gram_pieces(blocks, count_elem)
+    flip = 1
+    landed = paired(send, flip)
+    while 2 * flip < count_elem:
+        flip *= 2
+        keep, send = halve(keep, landed, flip)
+        landed = paired(send, flip)
+    margin = last_sum(keep, landed, local_count * count_elem * block)
     return (current, margin)
 
 

time: 81.3 us -> 75.6 us (0.930)
  local copies, waits for them, and re-layouts: 7.07 us -> 3.97 us
  waiting for transfers between devices: 40.8 us -> 38.1 us
    unnamed x18 -> x12, local copies, waits for them, and re-layouts: 7.07 us -> 3.97 us
    ppermute x5, waiting for transfers between devices: 31.9 us -> 30.3 us  [shifted(): lax.ppermute(block, axis, [((i - distance) % count, i) for i in range(cou...]
    ppermute x6 -> x4, waiting for transfers between devices: 8.89 us -> 7.81 us  [paired(): return lax.ppermute(block, 'elem', [(i, i ^ flip) for i in range(count)])]
    ppermute x6 -> x4, starting transfers between devices: 10.5 us -> 10.7 us  [paired(): return lax.ppermute(block, 'elem', [(i, i ^ flip) for i in range(count)])]
    pallas_call x3 -> x5, Pallas kernels: 2.47 us -> 2.54 us  [the longest x1 1.82 us: tables(): pl.pallas_call(body, name='tables', compiler_params=GRANT, in_specs=[SM,...]
  transfers between devices with their start and end apart: 11 -> 9, of which waited for: 8 -> 8; matrix products, arithmetic and copies ran while one was open for 0% -> 0% of each run, Pallas kernels for 2% -> 2%
where the time goes in v3:
time: 75.6 us; the launch traced here: 75.4 us
  waiting for transfers between devices  38.1 us (50%)
  starting transfers between devices  23 us (30%)
  Pallas kernels  9.71 us (13%)
  local copies, waits for them, and re-layouts  3.97 us (5%)
    ppermute x5, waiting for transfers between devices, shifted(): lax.ppermute(block, axis, [((i - distance) % count, i) for i in range(cou...  30.3 us
    ppermute x5, starting transfers between devices, shifted(): lax.ppermute(block, axis, [((i - distance) % count, i) for i in range(cou...  12.3 us
    ppermute x4, starting transfers between devices, paired(): return lax.ppermute(block, 'elem', [(i, i ^ flip) for i in range(count)])  10.7 us
    ppermute x4, waiting for transfers between devices, paired(): return lax.ppermute(block, 'elem', [(i, i ^ flip) for i in range(count)])  7.81 us
    pallas_call x2, Pallas kernels, degree_step(): pl.pallas_call(body, name='degree_last' if last else 'degree', compiler_p...  5.38 us
    unnamed x12, local copies, waits for them, and re-layouts  3.97 us
    pallas_call x1, Pallas kernels, tables(): pl.pallas_call(body, name='tables', compiler_params=GRANT, in_specs=[SM,...  1.82 us
  transfers between devices with their start and end apart: 9, of which 8 were waited for; matrix products, arithmetic and copies ran while one was open for 0% of the time, Pallas kernels for 2%

profile of v3, /device:TPU:0, one launch (start us, length us, event | category | flops | bytes accessed | tf_op | source)
XLA Modules:
  0.0 75.4 jit_solution(5166005668199718217)
XLA Ops:
  0.6 0.0 copy-start
  0.6 1.2 %copy-done = bf16[32,64,256]{2,1,0:T(8,128)(2,1)S(1)} copy-done((bf16[32,64,256]{2,1,0:T(8,128)(2,1)S(1)}, bf16[32,64,256]{2,1,0:T(8,128)(2,1)}, u32[]{:S(2)}) %copy-start) | copy-done | bytes 1048600
  1.9 0.0 copy-start.4
  1.9 0.7 copy-done.4
  2.5 0.0 copy-start.5
  2.5 0.7 copy-done.5
  3.2 0.0 copy-start.3
  3.2 1.0 %pack.1 = (bf16[16,64,256]{2,1,0:T(8,128)(2,1)S(1)}, bf16[16,64,256]{2,1,0:T(8,128)(2,1)S(1)}) custom-call(s32[4,32]{1,0:T(4,128)S(1)} %bitcast.4, s32[32]{0:T(128)S(1)} %copy-done.5, bf16[32,64,256]{2,1,0:T(8,128)(2,1)S(1)} %copy-done), custom_call_target="tpu_custom_call" | custom-call | tf_op jit(solution)/shard_map/pack/pallas_call | solution.py:65
  4.2 0.0 copy-start.1
  4.2 0.5 collective-permute-start
  4.7 5.0 %collective-permute-start.1 = (bf16[16,64,256]{2,1,0:T(8,128)(2,1)S(1)}, bf16[16,64,256]{2,1,0:T(8,128)(2,1)S(1)}, u32[]{:S(2)}, u32[]{:S(2)}) collective-permute-start(bf16[16,64,256]{2,1,0:T(8,128)(2,1)S(1)} %get-tuple-element.27), channel_id=1, source_target_pairs={{2,0},{4,2},{6,4},{8,6},{10,8},{12,10},{14,12},{16,14},{18,16},{20... | collective-permute-start | bytes 1572872 | tf_op jit(solution)/shard_map/ppermute | solution.py:21
  9.8 0.0 copy-done.3
  9.8 0.0 copy-start.2
  9.8 1.4 %copy-done.2 = bf16[32,64,320]{2,1,0:T(8,128)(2,1)S(1)} copy-done((bf16[32,64,320]{2,1,0:T(8,128)(2,1)S(1)}, bf16[32,64,320]{2,1,0:T(8,128)(2,1)}, u32[]{:S(2)}) %copy-start.2) | copy-done | bytes 1310744
  11.2 1.8 %tables.1 = (s32[128]{0:T(128)S(1)}, s32[33]{0:T(128)S(1)}, s32[32]{0:T(128)S(1)}, bf16[32,64,320]{2,1,0:T(8,128)(2,1)S(1)}, bf16[32,64,256]{2,1,0:T(8,128)(2,1)S(1)}) custom-call(s32[4,32]{1,0:T(4,128)S(1)} %bitcast.5, s32[32]{0:T(128)S(1)} %copy-done.5, bf16[32,64,320]{2,1,0:T(8,128)(2,1)S(1)} %copy-done.2, bf16[32,64,256]{2,1,0:T(8,128)(2,1)S(1)} %copy-done.3), custom_call_target="tpu_custom_call" | custom-call | tf_op jit(solution)/shard_map/tables/pallas_call | solution.py:111
  13.0 3.7 %collective-permute-done.from_prev = bf16[16,64,256]{2,1,0:T(8,128)(2,1)S(1)} collective-permute-done((bf16[16,64,256]{2,1,0:T(8,128)(2,1)S(1)}, bf16[16,64,256]{2,1,0:T(8,128)(2,1)S(1)}, u32[]{:S(2)}, u32[]{:S(2)}) %collective-permute-start) | collective-permute-done | bytes 524320 | tf_op jit(solution)/shard_map/ppermute | solution.py:21
  16.7 0.0 collective-permute-done.1.from_next
  16.7 0.0 copy-done.1
  16.7 2.2 %degree.1 = (bf16[32,64,256]{2,1,0:T(8,128)(2,1)S(1)}, bf16[16,64,256]{2,1,0:T(8,128)(2,1)S(1)}, bf16[16,64,256]{2,1,0:T(8,128)(2,1)S(1)}) custom-call(s32[128]{0:T(128)S(1)} %get-tuple-element.22.pool_index, s32[33]{0:T(128)S(1)} %get-tuple-element.23.orders, s32[32]{0:T(128)S(1)} %get-tuple-element.24.sizes, bf16[32,64,256]{2,1,0:T(8,128)(2,1)S(1)} %copy-done.1, ...), custom_call_target="tpu_custom_call" | custom-call | tf_op jit(solution)/shard_map/degree/pallas_call | solution.py:163
  18.9 4.9 %collective-permute-start.2 = (bf16[16,64,256]{2,1,0:T(8,128)(2,1)S(1)}, bf16[16,64,256]{2,1,0:T(8,128)(2,1)S(1)}, u32[]{:S(2)}, u32[]{:S(2)}) collective-permute-start(bf16[16,64,256]{2,1,0:T(8,128)(2,1)S(1)} %get-tuple-element.30), channel_id=1, source_target_pairs={{30,0},{0,2},{2,4},{4,6},{6,8},{8,10},{10,12},{12,14},{14,16},{16,... | collective-permute-start | bytes 1572872 | tf_op jit(solution)/shard_map/ppermute | solution.py:21
  23.9 0.0 collective-permute-start.3
  23.9 6.6 %collective-permute-done.2.from_prev = bf16[16,64,256]{2,1,0:T(8,128)(2,1)S(1)} collective-permute-done((bf16[16,64,256]{2,1,0:T(8,128)(2,1)S(1)}, bf16[16,64,256]{2,1,0:T(8,128)(2,1)S(1)}, u32[]{:S(2)}, u32[]{:S(2)}) %collective-permute-start.2) | collective-permute-done | bytes 524320 | tf_op jit(solution)/shard_map/ppermute | solution.py:21
  30.5 0.1 collective-permute-done.3.from_next
  30.6 3.2 %degree_last.1 = (bf16[32,64,256]{2,1,0:T(8,128)(2,1)}, bf16[32,64,256]{2,1,0:T(8,128)(2,1)S(1)}) custom-call(s32[128]{0:T(128)S(1)} %get-tuple-element.22.pool_index, s32[33]{0:T(128)S(1)} %get-tuple-element.23.orders, s32[32]{0:T(128)S(1)} %get-tuple-element.24.sizes, bf16[32,64,256]{2,1,0:T(8,128)(2,1)S(1)} %get-tuple-element.29.current, ...), custom_call_target="tpu_custom_call" | custom-call | tf_op jit(solution)/shard_map/degree_last/pallas_call | solution.py:163
  33.7 1.8 %collective-permute-start.4 = (bf16[2048,256]{1,0:T(8,128)(2,1)S(1)}, bf16[2048,256]{1,0:T(8,128)(2,1)S(1)}, u32[]{:S(2)}, u32[]{:S(2)}) collective-permute-start(bf16[2048,256]{1,0:T(8,128)(2,1)S(1)} %bitcast.2), channel_id=1, source_target_pairs={{1,0},{0,1},{3,2},{2,3},{5,4},{4,5},{7,6},{6,7},{9,8},{8,9},{11,10... | collective-permute-start | bytes 3145736 | tf_op jit(solution)/shard_map/ppermute | solution.py:21
  35.5 19.9 %collective-permute-done.4.refs_1_ = bf16[2048,256]{1,0:T(8,128)(2,1)S(1)} collective-permute-done((bf16[2048,256]{1,0:T(8,128)(2,1)S(1)}, bf16[2048,256]{1,0:T(8,128)(2,1)S(1)}, u32[]{:S(2)}, u32[]{:S(2)}) %collective-permute-start.4) | collective-permute-done | bytes 1048608 | tf_op jit(solution)/shard_map/ppermute | solution.py:21
  55.4 0.8 %gram.1 = (f32[8,32,256]{2,1,0:T(8,128)S(1)}, bf16[8,32,256]{2,1,0:T(8,128)(2,1)S(1)}) custom-call(bf16[2048,256]{1,0:T(8,128)(2,1)S(1)} %bitcast.3, bf16[2048,256]{1,0:T(8,128)(2,1)S(1)} %collective-permute-done.4.refs_1_), custom_call_target="tpu_custom_call" | custom-call | tf_op jit(solution)/shard_map/gram/pallas_call | solution.py:206
  56.2 4.3 %collective-permute-start.5 = (bf16[8,32,256]{2,1,0:T(8,128)(2,1)S(1)}, bf16[8,32,256]{2,1,0:T(8,128)(2,1)S(1)}, u32[]{:S(2)}, u32[]{:S(2)}) collective-permute-start(bf16[8,32,256]{2,1,0:T(8,128)(2,1)S(1)} %get-tuple-element.35), channel_id=1, source_target_pairs={{0,2},{2,0},{4,6},{6,4},{8,10},{10,8},{12,14},{14,12},{16,18},{18,... | collective-permute-start | bytes 393224 | tf_op jit(solution)/shard_map/ppermute | solution.py:251
  60.5 1.0 %collective-permute-done.5.landed = bf16[8,32,256]{2,1,0:T(8,128)(2,1)S(1)} collective-permute-done((bf16[8,32,256]{2,1,0:T(8,128)(2,1)S(1)}, bf16[8,32,256]{2,1,0:T(8,128)(2,1)S(1)}, u32[]{:S(2)}, u32[]{:S(2)}) %collective-permute-start.5) | collective-permute-done | bytes 131104 | tf_op jit(solution)/shard_map/ppermute | solution.py:251
  61.5 0.1 halve.3
  61.5 2.1 %collective-permute-start.6 = (bf16[4,32,256]{2,1,0:T(8,128)(2,1)S(1)}, bf16[4,32,256]{2,1,0:T(8,128)(2,1)S(1)}, u32[]{:S(2)}, u32[]{:S(2)}) collective-permute-start(bf16[4,32,256]{2,1,0:T(8,128)(2,1)S(1)} %get-tuple-element.37), channel_id=1, source_target_pairs={{0,4},{2,6},{4,0},{6,2},{8,12},{10,14},{12,8},{14,10},{16,20},{18,... | collective-permute-start | bytes 196616 | tf_op jit(solution)/shard_map/ppermute | solution.py:251
  63.7 2.4 %collective-permute-done.6.landed = bf16[4,32,256]{2,1,0:T(8,128)(2,1)S(1)} collective-permute-done((bf16[4,32,256]{2,1,0:T(8,128)(2,1)S(1)}, bf16[4,32,256]{2,1,0:T(8,128)(2,1)S(1)}, u32[]{:S(2)}, u32[]{:S(2)}) %collective-permute-start.6) | collective-permute-done | bytes 65568 | tf_op jit(solution)/shard_map/ppermute | solution.py:251
  66.1 1.6 %collective-permute-start.7 = (bf16[2,32,256]{2,1,0:T(8,128)(2,1)S(1)}, bf16[2,32,256]{2,1,0:T(8,128)(2,1)S(1)}, u32[]{:S(2)}, u32[]{:S(2)}) collective-permute-start(bf16[2,32,256]{2,1,0:T(8,128)(2,1)S(1)} %get-tuple-element.39), channel_id=1, source_target_pairs={{0,8},{2,10},{4,12},{6,14},{8,0},{10,2},{12,4},{14,6},{16,24},{18,... | collective-permute-start | bytes 98312 | tf_op jit(solution)/shard_map/ppermute | solution.py:251
  67.7 2.4 %collective-permute-done.7.landed = bf16[2,32,256]{2,1,0:T(8,128)(2,1)S(1)} collective-permute-done((bf16[2,32,256]{2,1,0:T(8,128)(2,1)S(1)}, bf16[2,32,256]{2,1,0:T(8,128)(2,1)S(1)}, u32[]{:S(2)}, u32[]{:S(2)}) %collective-permute-start.7) | collective-permute-done | bytes 32800 | tf_op jit(solution)/shard_map/ppermute | solution.py:251
  70.1 2.6 %collective-permute-start.8 = (bf16[1,32,256]{2,1,0:T(8,128)(2,1)S(1)}, bf16[1,32,256]{2,1,0:T(8,128)(2,1)S(1)}, u32[]{:S(2)}, u32[]{:S(2)}) collective-permute-start(bf16[1,32,256]{2,1,0:T(8,128)(2,1)S(1)} %get-tuple-element.41), channel_id=1, source_target_pairs={{0,16},{2,18},{4,20},{6,22},{8,24},{10,26},{12,28},{14,30},{16,0},... | collective-permute-start | bytes 49160 | tf_op jit(solution)/shard_map/ppermute | solution.py:251
  72.7 2.1 %collective-permute-done.8.landed = bf16[1,32,256]{2,1,0:T(8,128)(2,1)S(1)} collective-permute-done((bf16[1,32,256]{2,1,0:T(8,128)(2,1)S(1)}, bf16[1,32,256]{2,1,0:T(8,128)(2,1)S(1)}, u32[]{:S(2)}, u32[]{:S(2)}) %collective-permute-start.8) | collective-permute-done | bytes 16416 | tf_op jit(solution)/shard_map/ppermute | solution.py:251
  74.8 0.6 last_sum.1
  (2 shorter events, 0.0 us)
Async XLA Ops:
  0.6 1.2 %copy-start = (bf16[32,64,256]{2,1,0:T(8,128)(2,1)S(1)}, bf16[32,64,256]{2,1,0:T(8,128)(2,1)}, u32[]{:S(2)}) copy-start(bf16[32,64,256]{2,1,0:T(8,128)(2,1)} %previous.3) | copy-start | bytes 3145732
  1.9 0.7 copy-start.4
  2.5 0.7 copy-start.5
  3.2 6.6 %copy-start.3 = (bf16[32,64,256]{2,1,0:T(8,128)(2,1)S(1)}, bf16[32,64,256]{2,1,0:T(8,128)(2,1)}, u32[]{:S(2)}) copy-start(bf16[32,64,256]{2,1,0:T(8,128)(2,1)} %previous.2) | copy-start | bytes 3145732
  4.2 12.5 %copy-start.1 = (bf16[32,64,256]{2,1,0:T(8,128)(2,1)S(1)}, bf16[32,64,256]{2,1,0:T(8,128)(2,1)}, u32[]{:S(2)}) copy-start(bf16[32,64,256]{2,1,0:T(8,128)(2,1)} %previous.3) | copy-start | bytes 3145732
  4.2 12.5 %collective-permute-start = (bf16[16,64,256]{2,1,0:T(8,128)(2,1)S(1)}, bf16[16,64,256]{2,1,0:T(8,128)(2,1)S(1)}, u32[]{:S(2)}, u32[]{:S(2)}) collective-permute-start(bf16[16,64,256]{2,1,0:T(8,128)(2,1)S(1)} %get-tuple-element.26), channel_id=1, source_target_pairs={{30,0},{0,2},{2,4},{4,6},{6,8},{8,10},{10,12},{12,14},{14,16},{16,... | collective-permute-start | bytes 1572872 | tf_op jit(solution)/shard_map/ppermute | solution.py:21
  4.7 11.9 %collective-permute-start.1 = (bf16[16,64,256]{2,1,0:T(8,128)(2,1)S(1)}, bf16[16,64,256]{2,1,0:T(8,128)(2,1)S(1)}, u32[]{:S(2)}, u32[]{:S(2)}) collective-permute-start(bf16[16,64,256]{2,1,0:T(8,128)(2,1)S(1)} %get-tuple-element.27), channel_id=1, source_target_pairs={{2,0},{4,2},{6,4},{8,6},{10,8},{12,10},{14,12},{16,14},{18,16},{20... | collective-permute-start | bytes 1572872 | tf_op jit(solution)/shard_map/ppermute | solution.py:21
  9.8 1.4 %copy-start.2 = (bf16[32,64,320]{2,1,0:T(8,128)(2,1)S(1)}, bf16[32,64,320]{2,1,0:T(8,128)(2,1)}, u32[]{:S(2)}) copy-start(bf16[32,64,320]{2,1,0:T(8,128)(2,1)} %h_blocks.1) | copy-start | bytes 3932164
  18.9 11.5 %collective-permute-start.2 = (bf16[16,64,256]{2,1,0:T(8,128)(2,1)S(1)}, bf16[16,64,256]{2,1,0:T(8,128)(2,1)S(1)}, u32[]{:S(2)}, u32[]{:S(2)}) collective-permute-start(bf16[16,64,256]{2,1,0:T(8,128)(2,1)S(1)} %get-tuple-element.30), channel_id=1, source_target_pairs={{30,0},{0,2},{2,4},{4,6},{6,8},{8,10},{10,12},{12,14},{14,16},{16,... | collective-permute-start | bytes 1572872 | tf_op jit(solution)/shard_map/ppermute | solution.py:21
  23.9 6.7 %collective-permute-start.3 = (bf16[16,64,256]{2,1,0:T(8,128)(2,1)S(1)}, bf16[16,64,256]{2,1,0:T(8,128)(2,1)S(1)}, u32[]{:S(2)}, u32[]{:S(2)}) collective-permute-start(bf16[16,64,256]{2,1,0:T(8,128)(2,1)S(1)} %get-tuple-element.31), channel_id=1, source_target_pairs={{2,0},{4,2},{6,4},{8,6},{10,8},{12,10},{14,12},{16,14},{18,16},{20... | collective-permute-start | bytes 1572872 | tf_op jit(solution)/shard_map/ppermute | solution.py:21
  33.7 21.7 %collective-permute-start.4 = (bf16[2048,256]{1,0:T(8,128)(2,1)S(1)}, bf16[2048,256]{1,0:T(8,128)(2,1)S(1)}, u32[]{:S(2)}, u32[]{:S(2)}) collective-permute-start(bf16[2048,256]{1,0:T(8,128)(2,1)S(1)} %bitcast.2), channel_id=1, source_target_pairs={{1,0},{0,1},{3,2},{2,3},{5,4},{4,5},{7,6},{6,7},{9,8},{8,9},{11,10... | collective-permute-start | bytes 3145736 | tf_op jit(solution)/shard_map/ppermute | solution.py:21
  56.2 5.3 %collective-permute-start.5 = (bf16[8,32,256]{2,1,0:T(8,128)(2,1)S(1)}, bf16[8,32,256]{2,1,0:T(8,128)(2,1)S(1)}, u32[]{:S(2)}, u32[]{:S(2)}) collective-permute-start(bf16[8,32,256]{2,1,0:T(8,128)(2,1)S(1)} %get-tuple-element.35), channel_id=1, source_target_pairs={{0,2},{2,0},{4,6},{6,4},{8,10},{10,8},{12,14},{14,12},{16,18},{18,... | collective-permute-start | bytes 393224 | tf_op jit(solution)/shard_map/ppermute | solution.py:251
  61.5 4.6 %collective-permute-start.6 = (bf16[4,32,256]{2,1,0:T(8,128)(2,1)S(1)}, bf16[4,32,256]{2,1,0:T(8,128)(2,1)S(1)}, u32[]{:S(2)}, u32[]{:S(2)}) collective-permute-start(bf16[4,32,256]{2,1,0:T(8,128)(2,1)S(1)} %get-tuple-element.37), channel_id=1, source_target_pairs={{0,4},{2,6},{4,0},{6,2},{8,12},{10,14},{12,8},{14,10},{16,20},{18,... | collective-permute-start | bytes 196616 | tf_op jit(solution)/shard_map/ppermute | solution.py:251
  66.1 4.0 %collective-permute-start.7 = (bf16[2,32,256]{2,1,0:T(8,128)(2,1)S(1)}, bf16[2,32,256]{2,1,0:T(8,128)(2,1)S(1)}, u32[]{:S(2)}, u32[]{:S(2)}) collective-permute-start(bf16[2,32,256]{2,1,0:T(8,128)(2,1)S(1)} %get-tuple-element.39), channel_id=1, source_target_pairs={{0,8},{2,10},{4,12},{6,14},{8,0},{10,2},{12,4},{14,6},{16,24},{18,... | collective-permute-start | bytes 98312 | tf_op jit(solution)/shard_map/ppermute | solution.py:251
  70.1 4.7 %collective-permute-start.8 = (bf16[1,32,256]{2,1,0:T(8,128)(2,1)S(1)}, bf16[1,32,256]{2,1,0:T(8,128)(2,1)S(1)}, u32[]{:S(2)}, u32[]{:S(2)}) collective-permute-start(bf16[1,32,256]{2,1,0:T(8,128)(2,1)S(1)} %get-tuple-element.41), channel_id=1, source_target_pairs={{0,16},{2,18},{4,20},{6,22},{8,24},{10,26},{12,28},{14,30},{16,0},... | collective-permute-start | bytes 49160 | tf_op jit(solution)/shard_map/ppermute | solution.py:251

commit v4 on v3

--- a/solution.py
+++ b/solution.py
@@ -7,6 +7,7 @@
 
 GY = 16
 DEGREES = 2
+CHUNKS = 2
 
 center_value = 0.3
 spectral_half = 1.7
@@ -52,23 +53,28 @@
 def pack(values, sizes, near, count_elem):
     local_count, block, width = values.shape
 
-    def body(near, sizes, values, to_next, to_prev, orders):
+    part = width // CHUNKS
+
+    def body(near, sizes, values, *rest):
+        orders = rest[-1]
         bases = own_bases(local_count, count_elem)
         send_lists(near, orders, local_count, bases)
         rows = row_index(block, width)
         for s in range(GY):
-            for out, at in ((to_next, orders[s]), (to_prev, orders[GY + s])):
+            for way, at in enumerate((orders[s], orders[GY + s])):
                 held = values[at].astype(jnp.float32)
-                out[s] = jnp.where(rows < sizes[at], held, 0.0).astype(jnp.bfloat16)
-
-    halo = jax.ShapeDtypeStruct((GY, block, width), jnp.bfloat16)
+                masked = jnp.where(rows < sizes[at], held, 0.0).astype(jnp.bfloat16)
+                for c in range(CHUNKS):
+                    rest[2 * c + way][s] = masked[:, c * part : (c + 1) * part]
+
+    halo = jax.ShapeDtypeStruct((GY, block, part), jnp.bfloat16)
     return pl.pallas_call(
         body,
         name="pack",
         compiler_params=GRANT,
         in_specs=[SM, SM, VM],
-        out_specs=[VM, VM],
-        out_shape=[halo, halo],
+        out_specs=[VM] * (2 * CHUNKS),
+        out_shape=[halo] * (2 * CHUNKS),
         scratch_shapes=[pltpu.SMEM((2 * GY + 1,), jnp.int32)],
     )(near, sizes, values)
 
@@ -128,14 +134,21 @@
     )(near, sizes, h_blocks, previous)
 
 
-def degree_step(pool_index, orders, sizes, current, previous, from_prev, from_next, h_blocks, last):
-    local_count, block, width = current.shape
+def degree_step(pool_index, orders, sizes, current, previous, from_prev, from_next, h_blocks, chunk, last):
+    local_count, block, _ = current.shape
+    width = from_prev.shape[2]
+
+    def lanes(values):
+        low = chunk * width if values.shape[2] > width else 0
+        return slice(low, low + width)
+
+    at_current, at_previous = lanes(current), lanes(previous)
 
     def body(pool_index, orders, sizes, current, previous, from_prev, from_next, h_blocks, following, *rest):
         pool = rest[-1]
         rows = row_index(block, width)
         for i in range(local_count):
-            held = current[i].astype(jnp.float32)
+            held = current[i, :, at_current].astype(jnp.float32)
             pool[i] = jnp.where(rows < sizes[i], held, 0.0).astype(jnp.bfloat16)
         pool[local_count : local_count + GY] = from_prev[...]
         pool[local_count + GY :] = from_next[...]
@@ -147,19 +160,17 @@
             applied = jnp.dot(h_blocks[i], stacked, preferred_element_type=jnp.float32)
             value = 2.0 / spectral_half * (
                 applied - center_value * own.astype(jnp.float32)
-            ) - previous[i].astype(jnp.float32)
+            ) - previous[i, :, at_previous].astype(jnp.float32)
             following[i] = jnp.where(rows < sizes[i], value, 0.0).astype(jnp.bfloat16)
-        if last:
-            rest[0][...] = following[...]
-        else:
+        if not last:
             to_next, to_prev = rest[:2]
             for s in range(GY):
                 to_next[s] = following[orders[s]]
                 to_prev[s] = following[orders[GY + s]]
 
-    whole = jax.ShapeDtypeStruct(current.shape, jnp.bfloat16)
+    whole = jax.ShapeDtypeStruct((local_count, block, width), jnp.bfloat16)
     halo = jax.ShapeDtypeStruct((GY, block, width), jnp.bfloat16)
-    outs = [whole, whole] if last else [whole, halo, halo]
+    outs = [whole] if last else [whole, halo, halo]
     return pl.pallas_call(
         body,
         name="degree_last" if last else "degree",
@@ -182,20 +193,41 @@
     return [jax.ShapeDtypeStruct(piece, jnp.float32), jax.ShapeDtypeStruct(piece, jnp.bfloat16)]
 
 
+def join(chunks):
+    local_count, block, part = chunks[0].shape
+
+    def body(*refs):
+        for c in range(CHUNKS):
+            refs[-1][:, :, c * part : (c + 1) * part] = refs[c][...]
+
+    return pl.pallas_call(
+        body,
+        name="join",
+        compiler_params=GRANT,
+        in_specs=[VM] * CHUNKS,
+        out_specs=VM,
+        out_shape=jax.ShapeDtypeStruct((local_count, block, part * CHUNKS), jnp.bfloat16),
+    )(*chunks)
+
+
 def gram_pieces(blocks, count_elem):
-    depth, width = blocks[0].shape
-    count_band = len(blocks)
+    width = CHUNKS * blocks[0].shape[1]
+    count_band = len(blocks) // CHUNKS
     rows = count_band * width // count_elem
     per_band = width // rows
 
     def body(*refs):
-        ins, keep, send, whole = refs[:count_band], *refs[count_band:]
+        ins, keep, send, whole = refs[: len(blocks)], *refs[len(blocks) :]
+        sides = [
+            jnp.concatenate([ref[...] for ref in ins[CHUNKS * k : CHUNKS * (k + 1)]], axis=1)
+            for k in range(count_band)
+        ]
         band = lax.axis_index("band")
         for step in range(count_band):
             source = lax.rem(band - step + count_band, count_band)
             product = lax.dot_general(
-                ins[step][...],
-                ins[0][...],
+                sides[step],
+                sides[0],
                 (((0,), (0,)), ((), ())),
                 preferred_element_type=jnp.float32,
             )
@@ -207,7 +239,7 @@
         body,
         name="gram",
         compiler_params=GRANT,
-        in_specs=[VM] * count_band,
+        in_specs=[VM] * len(blocks),
         out_specs=[VM, VM],
         out_shape=split_shapes(count_elem, rows, width),
         scratch_shapes=[pltpu.VMEM((count_elem, rows, width), jnp.float32)],
@@ -255,26 +287,31 @@
     local_count, block, band_width = y_current.shape
     count_elem = lax.axis_size("elem")
     count_band = lax.axis_size("band")
-    current, previous = y_current, y_previous
     neighbours = neighbours.T
-    to_next, to_prev = pack(current, basis_sizes, neighbours, count_elem)
-    pool_index, orders, sizes, h_blocks, previous = tables(
-        neighbours, basis_sizes, h_blocks, previous, count_elem
+    halos = pack(y_current, basis_sizes, neighbours, count_elem)
+    halos = [halos[2 * c : 2 * c + 2] for c in range(CHUNKS)]
+    pool_index, orders, sizes, h_blocks, y_previous = tables(
+        neighbours, basis_sizes, h_blocks, y_previous, count_elem
     )
+    current, previous = [y_current] * CHUNKS, [y_previous] * CHUNKS
+    moved = []
     for degree in range(DEGREES):
-        from_prev = shifted(to_next, "elem", 1)
-        from_next = shifted(to_prev, "elem", -1)
         last = degree == DEGREES - 1
-        result = degree_step(
-            pool_index, orders, sizes, current, previous, from_prev, from_next, h_blocks, last
-        )
-        previous = current
-        current = result[0]
-        if not last:
-            to_next, to_prev = result[1:]
-    flat = result[1]
-    flat = flat.reshape(local_count * block, band_width)
-    blocks = [flat] + [shifted(flat, "band", step) for step in range(1, count_band)]
+        arrived = [
+            (shifted(to_next, "elem", 1), shifted(to_prev, "elem", -1)) for to_next, to_prev in halos
+        ]
+        for c in range(CHUNKS):
+            result = degree_step(
+                pool_index, orders, sizes, current[c], previous[c], *arrived[c], h_blocks, c, last
+            )
+            previous[c], current[c] = current[c], result[0]
+            if last:
+                flat = result[0].reshape(local_count * block, band_width // CHUNKS)
+                moved.append([flat] + [shifted(flat, "band", step) for step in range(1, count_band)])
+            else:
+                halos[c] = result[1:]
+    blocks = [moved[c][step] for step in range(count_band) for c in range(CHUNKS)]
+    filtered = join(current)
     keep, send = gram_pieces(blocks, count_elem)
     flip = 1
     landed = paired(send, flip)
@@ -283,7 +320,7 @@
         keep, send = halve(keep, landed, flip)
         landed = paired(send, flip)
     margin = last_sum(keep, landed, local_count * count_elem * block)
-    return (current, margin)
+    return (filtered, margin)
 
 
 def solution(mesh):

time: 75.6 us -> 71.7 us (0.948)
  waiting for transfers between devices: 38.1 us -> 31.5 us
  Pallas kernels: 9.71 us -> 11.1 us
  starting transfers between devices: 23 us -> 24 us
    ppermute x5 -> x10, waiting for transfers between devices: 30.3 us -> 19.4 us  [shifted(): lax.ppermute(block, axis, [((i - distance) % count, i) for i in range(cou...]
    ppermute x5 -> x10, starting transfers between devices: 12.3 us -> 22.9 us  [shifted(): lax.ppermute(block, axis, [((i - distance) % count, i) for i in range(cou...]
    ppermute x4, starting transfers between devices: 10.7 us -> 1.14 us  [paired(): return lax.ppermute(block, 'elem', [(i, i ^ flip) for i in range(count)])]
    ppermute x4, waiting for transfers between devices: 7.81 us -> 12.1 us  [paired(): return lax.ppermute(block, 'elem', [(i, i ^ flip) for i in range(count)])]
    pallas_call x0 -> x1, Pallas kernels: none -> 1.15 us  [join(): pl.pallas_call(body, name='join', compiler_params=GRANT, in_specs=[VM] *...]
    pallas_call x2 -> x4, Pallas kernels: 5.38 us -> 5.64 us  [degree_step(): pl.pallas_call(body, name='degree_last' if last else 'degree', compiler_p...]
  transfers between devices with their start and end apart: 9 -> 14, of which waited for: 8 -> 7; matrix products, arithmetic and copies ran while one was open for 0% -> 0% of each run, Pallas kernels for 2% -> 12%
where the time goes in v4:
time: 71.7 us; the launch traced here: 71.4 us
  waiting for transfers between devices  31.5 us (44%)
  starting transfers between devices  24 us (33%)
  Pallas kernels  11.1 us (15%)
  local copies, waits for them, and re-layouts  3.97 us (6%)
  between operations  0.78 us (1%)
    ppermute x10, starting transfers between devices, shifted(): lax.ppermute(block, axis, [((i - distance) % count, i) for i in range(cou...  22.9 us
    ppermute x10, waiting for transfers between devices, shifted(): lax.ppermute(block, axis, [((i - distance) % count, i) for i in range(cou...  19.4 us
    ppermute x4, waiting for transfers between devices, paired(): return lax.ppermute(block, 'elem', [(i, i ^ flip) for i in range(count)])  12.1 us
    pallas_call x4, Pallas kernels, degree_step(): pl.pallas_call(body, name='degree_last' if last else 'degree', compiler_p...  5.64 us
    unnamed x12, local copies, waits for them, and re-layouts  3.97 us
    pallas_call x1, Pallas kernels, tables(): pl.pallas_call(body, name='tables', compiler_params=GRANT, in_specs=[SM,...  1.82 us
  transfers between devices with their start and end apart: 14, of which 7 were waited for; matrix products, arithmetic and copies ran while one was open for 0% of the time, Pallas kernels for 12%

profile of v4, /device:TPU:0, one launch (start us, length us, event | category | flops | bytes accessed | tf_op | source)
XLA Modules:
  0.0 71.4 jit_solution(11135595248946545694)
XLA Ops:
  0.6 0.0 copy-start
  0.6 1.2 %copy-done = bf16[32,64,256]{2,1,0:T(8,128)(2,1)S(1)} copy-done((bf16[32,64,256]{2,1,0:T(8,128)(2,1)S(1)}, bf16[32,64,256]{2,1,0:T(8,128)(2,1)}, u32[]{:S(2)}) %copy-start) | copy-done | bytes 1048600
  1.9 0.0 copy-start.4
  1.9 0.7 copy-done.4
  2.5 0.0 copy-start.5
  2.5 0.7 copy-done.5
  3.2 0.0 copy-start.3
  3.2 1.0 %pack.1 = (bf16[16,64,128]{2,1,0:T(8,128)(2,1)S(1)}, bf16[16,64,128]{2,1,0:T(8,128)(2,1)S(1)}, bf16[16,64,128]{2,1,0:T(8,128)(2,1)S(1)}, bf16[16,64,128]{2,1,0:T(8,128)(2,1)S(1)}) custom-call(s32[4,32]{1,0:T(4,128)S(1)} %bitcast.7, s32[32]{0:T(128)S(1)} %copy-done.5, bf16[32,64,256]{2,1,0:T(8,128)(2,1)S(1)} %copy-done), custom_call_target="tpu_custom_call" | custom-call | tf_op jit(solution)/shard_map/pack/pallas_call | solution.py:71
  4.2 0.0 copy-start.1
  4.2 0.5 collective-permute-start
  4.7 5.0 %collective-permute-start.1 = (bf16[16,64,128]{2,1,0:T(8,128)(2,1)S(1)}, bf16[16,64,128]{2,1,0:T(8,128)(2,1)S(1)}, u32[]{:S(2)}, u32[]{:S(2)}) collective-permute-start(bf16[16,64,128]{2,1,0:T(8,128)(2,1)S(1)} %get-tuple-element.30), channel_id=1, source_target_pairs={{2,0},{4,2},{6,4},{8,6},{10,8},{12,10},{14,12},{16,14},{18,16},{20... | collective-permute-start | bytes 786440 | tf_op jit(solution)/shard_map/ppermute | solution.py:22
  9.8 0.0 collective-permute-start.4
  9.8 4.4 %collective-permute-start.5 = (bf16[16,64,128]{2,1,0:T(8,128)(2,1)S(1)}, bf16[16,64,128]{2,1,0:T(8,128)(2,1)S(1)}, u32[]{:S(2)}, u32[]{:S(2)}) collective-permute-start(bf16[16,64,128]{2,1,0:T(8,128)(2,1)S(1)} %get-tuple-element.36), channel_id=1, source_target_pairs={{2,0},{4,2},{6,4},{8,6},{10,8},{12,10},{14,12},{16,14},{18,16},{20... | collective-permute-start | bytes 786440 | tf_op jit(solution)/shard_map/ppermute | solution.py:22
  14.2 0.0 copy-done.3
  14.2 0.0 copy-start.2
  14.2 1.4 %copy-done.2 = bf16[32,64,320]{2,1,0:T(8,128)(2,1)S(1)} copy-done((bf16[32,64,320]{2,1,0:T(8,128)(2,1)S(1)}, bf16[32,64,320]{2,1,0:T(8,128)(2,1)}, u32[]{:S(2)}) %copy-start.2) | copy-done | bytes 1310744
  15.6 1.8 %tables.1 = (s32[128]{0:T(128)S(1)}, s32[33]{0:T(128)S(1)}, s32[32]{0:T(128)S(1)}, bf16[32,64,320]{2,1,0:T(8,128)(2,1)S(1)}, bf16[32,64,256]{2,1,0:T(8,128)(2,1)S(1)}) custom-call(s32[4,32]{1,0:T(4,128)S(1)} %bitcast.8, s32[32]{0:T(128)S(1)} %copy-done.5, bf16[32,64,320]{2,1,0:T(8,128)(2,1)S(1)} %copy-done.2, bf16[32,64,256]{2,1,0:T(8,128)(2,1)S(1)} %copy-done.3), custom_call_target="tpu_custom_call" | custom-call | tf_op jit(solution)/shard_map/tables/pallas_call | solution.py:117
  17.5 0.0 collective-permute-done.from_prev
  17.5 0.0 collective-permute-done.1.from_next
  17.5 0.0 copy-done.1
  17.5 1.4 %degree.2 = (bf16[32,64,128]{2,1,0:T(8,128)(2,1)S(1)}, bf16[16,64,128]{2,1,0:T(8,128)(2,1)S(1)}, bf16[16,64,128]{2,1,0:T(8,128)(2,1)S(1)}) custom-call(s32[128]{0:T(128)S(1)} %get-tuple-element.25.pool_index, s32[33]{0:T(128)S(1)} %get-tuple-element.26.orders, s32[32]{0:T(128)S(1)} %get-tuple-element.27.sizes, bf16[32,64,256]{2,1,0:T(8,128)(2,1)S(1)} %copy-done.1, ...), custom_call_target="tpu_custom_call" | custom-call | tf_op jit(solution)/shard_map/degree/pallas_call | solution.py:174
  18.9 1.3 %collective-permute-start.2 = (bf16[16,64,128]{2,1,0:T(8,128)(2,1)S(1)}, bf16[16,64,128]{2,1,0:T(8,128)(2,1)S(1)}, u32[]{:S(2)}, u32[]{:S(2)}) collective-permute-start(bf16[16,64,128]{2,1,0:T(8,128)(2,1)S(1)} %get-tuple-element.33), channel_id=1, source_target_pairs={{30,0},{0,2},{2,4},{4,6},{6,8},{8,10},{10,12},{12,14},{14,16},{16,... | collective-permute-start | bytes 786440 | tf_op jit(solution)/shard_map/ppermute | solution.py:22
  20.3 3.2 %collective-permute-start.3 = (bf16[16,64,128]{2,1,0:T(8,128)(2,1)S(1)}, bf16[16,64,128]{2,1,0:T(8,128)(2,1)S(1)}, u32[]{:S(2)}, u32[]{:S(2)}) collective-permute-start(bf16[16,64,128]{2,1,0:T(8,128)(2,1)S(1)} %get-tuple-element.34), channel_id=1, source_target_pairs={{2,0},{4,2},{6,4},{8,6},{10,8},{12,10},{14,12},{16,14},{18,16},{20... | collective-permute-start | bytes 786440 | tf_op jit(solution)/shard_map/ppermute | solution.py:22
  23.4 0.0 collective-permute-done.4.from_prev
  23.4 0.0 collective-permute-done.5.from_next
  23.4 1.4 %degree.3 = (bf16[32,64,128]{2,1,0:T(8,128)(2,1)S(1)}, bf16[16,64,128]{2,1,0:T(8,128)(2,1)S(1)}, bf16[16,64,128]{2,1,0:T(8,128)(2,1)S(1)}) custom-call(s32[128]{0:T(128)S(1)} %get-tuple-element.25.pool_index, s32[33]{0:T(128)S(1)} %get-tuple-element.26.orders, s32[32]{0:T(128)S(1)} %get-tuple-element.27.sizes, bf16[32,64,256]{2,1,0:T(8,128)(2,1)S(1)} %copy-done.1, ...), custom_call_target="tpu_custom_call" | custom-call | tf_op jit(solution)/shard_map/degree/pallas_call | solution.py:174
  24.9 0.1 collective-permute-start.6
  24.9 4.4 %collective-permute-start.7 = (bf16[16,64,128]{2,1,0:T(8,128)(2,1)S(1)}, bf16[16,64,128]{2,1,0:T(8,128)(2,1)S(1)}, u32[]{:S(2)}, u32[]{:S(2)}) collective-permute-start(bf16[16,64,128]{2,1,0:T(8,128)(2,1)S(1)} %get-tuple-element.39), channel_id=1, source_target_pairs={{2,0},{4,2},{6,4},{8,6},{10,8},{12,10},{14,12},{16,14},{18,16},{20... | collective-permute-start | bytes 786440 | tf_op jit(solution)/shard_map/ppermute | solution.py:22
  29.4 0.0 collective-permute-done.2.from_prev
  29.4 0.0 collective-permute-done.3.from_next
  29.4 1.4 %degree_last.2.refs_0_ = bf16[32,64,128]{2,1,0:T(8,128)(2,1)S(1)} custom-call(s32[128]{0:T(128)S(1)} %get-tuple-element.25.pool_index, s32[33]{0:T(128)S(1)} %get-tuple-element.26.orders, s32[32]{0:T(128)S(1)} %get-tuple-element.27.sizes, bf16[32,64,128]{2,1,0:T(8,128)(2,1)S(1)} %get-tuple-element.32.current, bf16[32,64,256]{2,1,0:T(8,128)(2,1)S(1)} %copy-done.1, ...), custom_call_target="tpu_custom_call" | custom-call | tf_op jit(solution)/shard_map/degree_last/pallas_call | solution.py:174
  30.8 1.9 %collective-permute-start.8 = (bf16[2048,128]{1,0:T(8,128)(2,1)S(1)}, bf16[2048,128]{1,0:T(8,128)(2,1)S(1)}, u32[]{:S(2)}, u32[]{:S(2)}) collective-permute-start(bf16[2048,128]{1,0:T(8,128)(2,1)S(1)} %bitcast.3), channel_id=1, source_target_pairs={{1,0},{0,1},{3,2},{2,3},{5,4},{4,5},{7,6},{6,7},{9,8},{8,9},{11,10... | collective-permute-start | bytes 1572872 | tf_op jit(solution)/shard_map/ppermute | solution.py:22
  32.7 0.8 %collective-permute-done.6.from_prev = bf16[16,64,128]{2,1,0:T(8,128)(2,1)S(1)} collective-permute-done((bf16[16,64,128]{2,1,0:T(8,128)(2,1)S(1)}, bf16[16,64,128]{2,1,0:T(8,128)(2,1)S(1)}, u32[]{:S(2)}, u32[]{:S(2)}) %collective-permute-start.6) | collective-permute-done | bytes 262176 | tf_op jit(solution)/shard_map/ppermute | solution.py:22
  33.5 0.0 collective-permute-done.7.from_next
  33.5 1.4 %degree_last.3.refs_1_ = bf16[32,64,128]{2,1,0:T(8,128)(2,1)S(1)} custom-call(s32[128]{0:T(128)S(1)} %get-tuple-element.25.pool_index, s32[33]{0:T(128)S(1)} %get-tuple-element.26.orders, s32[32]{0:T(128)S(1)} %get-tuple-element.27.sizes, bf16[32,64,128]{2,1,0:T(8,128)(2,1)S(1)} %get-tuple-element.37.current, bf16[32,64,256]{2,1,0:T(8,128)(2,1)S(1)} %copy-done.1, ...), custom_call_target="tpu_custom_call" | custom-call | tf_op jit(solution)/shard_map/degree_last/pallas_call | solution.py:174
  34.9 1.9 %collective-permute-start.9 = (bf16[2048,128]{1,0:T(8,128)(2,1)S(1)}, bf16[2048,128]{1,0:T(8,128)(2,1)S(1)}, u32[]{:S(2)}, u32[]{:S(2)}) collective-permute-start(bf16[2048,128]{1,0:T(8,128)(2,1)S(1)} %bitcast.5), channel_id=1, source_target_pairs={{1,0},{0,1},{3,2},{2,3},{5,4},{4,5},{7,6},{6,7},{9,8},{8,9},{11,10... | collective-permute-start | bytes 1572872 | tf_op jit(solution)/shard_map/ppermute | solution.py:22
  36.9 8.8 %collective-permute-done.8.refs_2_ = bf16[2048,128]{1,0:T(8,128)(2,1)S(1)} collective-permute-done((bf16[2048,128]{1,0:T(8,128)(2,1)S(1)}, bf16[2048,128]{1,0:T(8,128)(2,1)S(1)}, u32[]{:S(2)}, u32[]{:S(2)}) %collective-permute-start.8) | collective-permute-done | bytes 524320 | tf_op jit(solution)/shard_map/ppermute | solution.py:22
  45.6 9.8 %collective-permute-done.9.refs_3_ = bf16[2048,128]{1,0:T(8,128)(2,1)S(1)} collective-permute-done((bf16[2048,128]{1,0:T(8,128)(2,1)S(1)}, bf16[2048,128]{1,0:T(8,128)(2,1)S(1)}, u32[]{:S(2)}, u32[]{:S(2)}) %collective-permute-start.9) | collective-permute-done | bytes 524320 | tf_op jit(solution)/shard_map/ppermute | solution.py:22
  55.5 0.8 %gram.1 = (f32[8,32,256]{2,1,0:T(8,128)S(1)}, bf16[8,32,256]{2,1,0:T(8,128)(2,1)S(1)}) custom-call(bf16[2048,128]{1,0:T(8,128)(2,1)S(1)} %bitcast.4, bf16[2048,128]{1,0:T(8,128)(2,1)S(1)} %bitcast.6, bf16[2048,128]{1,0:T(8,128)(2,1)S(1)} %collective-permute-done.8.refs_2_, bf16[2048,128]{1,0:T(8,128)(2,1)S(1)} %collective-permute-done.9.refs_3_), custom_call_target="tpu_custom_call" | custom-call | tf_op jit(solution)/shard_map/gram/pallas_call | solution.py:238
  56.3 0.1 collective-permute-start.10
  56.4 1.3 %collective-permute-done.10.landed = bf16[8,32,256]{2,1,0:T(8,128)(2,1)S(1)} collective-permute-done((bf16[8,32,256]{2,1,0:T(8,128)(2,1)S(1)}, bf16[8,32,256]{2,1,0:T(8,128)(2,1)S(1)}, u32[]{:S(2)}, u32[]{:S(2)}) %collective-permute-start.10) | collective-permute-done | bytes 131104 | tf_op jit(solution)/shard_map/ppermute | solution.py:283
  57.7 0.1 halve.3
  57.7 0.1 collective-permute-start.11
  57.8 4.3 %collective-permute-done.11.landed = bf16[4,32,256]{2,1,0:T(8,128)(2,1)S(1)} collective-permute-done((bf16[4,32,256]{2,1,0:T(8,128)(2,1)S(1)}, bf16[4,32,256]{2,1,0:T(8,128)(2,1)S(1)}, u32[]{:S(2)}, u32[]{:S(2)}) %collective-permute-start.11) | collective-permute-done | bytes 65568 | tf_op jit(solution)/shard_map/ppermute | solution.py:283
  62.1 0.1 collective-permute-start.12
  62.2 3.9 %collective-permute-done.12.landed = bf16[2,32,256]{2,1,0:T(8,128)(2,1)S(1)} collective-permute-done((bf16[2,32,256]{2,1,0:T(8,128)(2,1)S(1)}, bf16[2,32,256]{2,1,0:T(8,128)(2,1)S(1)}, u32[]{:S(2)}, u32[]{:S(2)}) %collective-permute-start.12) | collective-permute-done | bytes 32800 | tf_op jit(solution)/shard_map/ppermute | solution.py:283
  66.1 0.9 %collective-permute-start.13 = (bf16[1,32,256]{2,1,0:T(8,128)(2,1)S(1)}, bf16[1,32,256]{2,1,0:T(8,128)(2,1)S(1)}, u32[]{:S(2)}, u32[]{:S(2)}) collective-permute-start(bf16[1,32,256]{2,1,0:T(8,128)(2,1)S(1)} %get-tuple-element.47), channel_id=1, source_target_pairs={{0,16},{2,18},{4,20},{6,22},{8,24},{10,26},{12,28},{14,30},{16,0},... | collective-permute-start | bytes 49160 | tf_op jit(solution)/shard_map/ppermute | solution.py:283
  67.0 1.1 %join.1 = bf16[32,64,256]{2,1,0:T(8,128)(2,1)} custom-call(bf16[32,64,128]{2,1,0:T(8,128)(2,1)S(1)} %degree_last.2.refs_0_, bf16[32,64,128]{2,1,0:T(8,128)(2,1)S(1)} %degree_last.3.refs_1_), custom_call_target="tpu_custom_call" | custom-call | tf_op jit(solution)/shard_map/join/pallas_call | solution.py:203
  68.2 2.6 %collective-permute-done.13.landed = bf16[1,32,256]{2,1,0:T(8,128)(2,1)S(1)} collective-permute-done((bf16[1,32,256]{2,1,0:T(8,128)(2,1)S(1)}, bf16[1,32,256]{2,1,0:T(8,128)(2,1)S(1)}, u32[]{:S(2)}, u32[]{:S(2)}) %collective-permute-start.13) | collective-permute-done | bytes 16416 | tf_op jit(solution)/shard_map/ppermute | solution.py:283
  70.8 0.6 last_sum.1
  (2 shorter events, 0.0 us)
Async XLA Ops:
  0.6 1.2 %copy-start = (bf16[32,64,256]{2,1,0:T(8,128)(2,1)S(1)}, bf16[32,64,256]{2,1,0:T(8,128)(2,1)}, u32[]{:S(2)}) copy-start(bf16[32,64,256]{2,1,0:T(8,128)(2,1)} %previous.5) | copy-start | bytes 3145732
  1.9 0.7 copy-start.4
  2.5 0.7 copy-start.5
  3.2 11.0 %copy-start.3 = (bf16[32,64,256]{2,1,0:T(8,128)(2,1)S(1)}, bf16[32,64,256]{2,1,0:T(8,128)(2,1)}, u32[]{:S(2)}) copy-start(bf16[32,64,256]{2,1,0:T(8,128)(2,1)} %previous.3) | copy-start | bytes 3145732
  4.2 13.3 %copy-start.1 = (bf16[32,64,256]{2,1,0:T(8,128)(2,1)S(1)}, bf16[32,64,256]{2,1,0:T(8,128)(2,1)}, u32[]{:S(2)}) copy-start(bf16[32,64,256]{2,1,0:T(8,128)(2,1)} %previous.5) | copy-start | bytes 3145732
  4.2 13.3 %collective-permute-start = (bf16[16,64,128]{2,1,0:T(8,128)(2,1)S(1)}, bf16[16,64,128]{2,1,0:T(8,128)(2,1)S(1)}, u32[]{:S(2)}, u32[]{:S(2)}) collective-permute-start(bf16[16,64,128]{2,1,0:T(8,128)(2,1)S(1)} %get-tuple-element.29), channel_id=1, source_target_pairs={{30,0},{0,2},{2,4},{4,6},{6,8},{8,10},{10,12},{12,14},{14,16},{16,... | collective-permute-start | bytes 786440 | tf_op jit(solution)/shard_map/ppermute | solution.py:22
  4.7 12.7 %collective-permute-start.1 = (bf16[16,64,128]{2,1,0:T(8,128)(2,1)S(1)}, bf16[16,64,128]{2,1,0:T(8,128)(2,1)S(1)}, u32[]{:S(2)}, u32[]{:S(2)}) collective-permute-start(bf16[16,64,128]{2,1,0:T(8,128)(2,1)S(1)} %get-tuple-element.30), channel_id=1, source_target_pairs={{2,0},{4,2},{6,4},{8,6},{10,8},{12,10},{14,12},{16,14},{18,16},{20... | collective-permute-start | bytes 786440 | tf_op jit(solution)/shard_map/ppermute | solution.py:22
  9.8 13.6 %collective-permute-start.4 = (bf16[16,64,128]{2,1,0:T(8,128)(2,1)S(1)}, bf16[16,64,128]{2,1,0:T(8,128)(2,1)S(1)}, u32[]{:S(2)}, u32[]{:S(2)}) collective-permute-start(bf16[16,64,128]{2,1,0:T(8,128)(2,1)S(1)} %get-tuple-element.35), channel_id=1, source_target_pairs={{30,0},{0,2},{2,4},{4,6},{6,8},{8,10},{10,12},{12,14},{14,16},{16,... | collective-permute-start | bytes 786440 | tf_op jit(solution)/shard_map/ppermute | solution.py:22
  9.8 13.6 %collective-permute-start.5 = (bf16[16,64,128]{2,1,0:T(8,128)(2,1)S(1)}, bf16[16,64,128]{2,1,0:T(8,128)(2,1)S(1)}, u32[]{:S(2)}, u32[]{:S(2)}) collective-permute-start(bf16[16,64,128]{2,1,0:T(8,128)(2,1)S(1)} %get-tuple-element.36), channel_id=1, source_target_pairs={{2,0},{4,2},{6,4},{8,6},{10,8},{12,10},{14,12},{16,14},{18,16},{20... | collective-permute-start | bytes 786440 | tf_op jit(solution)/shard_map/ppermute | solution.py:22
  14.2 1.4 %copy-start.2 = (bf16[32,64,320]{2,1,0:T(8,128)(2,1)S(1)}, bf16[32,64,320]{2,1,0:T(8,128)(2,1)}, u32[]{:S(2)}) copy-start(bf16[32,64,320]{2,1,0:T(8,128)(2,1)} %h_blocks.1) | copy-start | bytes 3932164
  18.9 10.4 %collective-permute-start.2 = (bf16[16,64,128]{2,1,0:T(8,128)(2,1)S(1)}, bf16[16,64,128]{2,1,0:T(8,128)(2,1)S(1)}, u32[]{:S(2)}, u32[]{:S(2)}) collective-permute-start(bf16[16,64,128]{2,1,0:T(8,128)(2,1)S(1)} %get-tuple-element.33), channel_id=1, source_target_pairs={{30,0},{0,2},{2,4},{4,6},{6,8},{8,10},{10,12},{12,14},{14,16},{16,... | collective-permute-start | bytes 786440 | tf_op jit(solution)/shard_map/ppermute | solution.py:22
  20.3 9.1 %collective-permute-start.3 = (bf16[16,64,128]{2,1,0:T(8,128)(2,1)S(1)}, bf16[16,64,128]{2,1,0:T(8,128)(2,1)S(1)}, u32[]{:S(2)}, u32[]{:S(2)}) collective-permute-start(bf16[16,64,128]{2,1,0:T(8,128)(2,1)S(1)} %get-tuple-element.34), channel_id=1, source_target_pairs={{2,0},{4,2},{6,4},{8,6},{10,8},{12,10},{14,12},{16,14},{18,16},{20... | collective-permute-start | bytes 786440 | tf_op jit(solution)/shard_map/ppermute | solution.py:22
  24.9 8.7 %collective-permute-start.6 = (bf16[16,64,128]{2,1,0:T(8,128)(2,1)S(1)}, bf16[16,64,128]{2,1,0:T(8,128)(2,1)S(1)}, u32[]{:S(2)}, u32[]{:S(2)}) collective-permute-start(bf16[16,64,128]{2,1,0:T(8,128)(2,1)S(1)} %get-tuple-element.38), channel_id=1, source_target_pairs={{30,0},{0,2},{2,4},{4,6},{6,8},{8,10},{10,12},{12,14},{14,16},{16,... | collective-permute-start | bytes 786440 | tf_op jit(solution)/shard_map/ppermute | solution.py:22
  24.9 8.6 %collective-permute-start.7 = (bf16[16,64,128]{2,1,0:T(8,128)(2,1)S(1)}, bf16[16,64,128]{2,1,0:T(8,128)(2,1)S(1)}, u32[]{:S(2)}, u32[]{:S(2)}) collective-permute-start(bf16[16,64,128]{2,1,0:T(8,128)(2,1)S(1)} %get-tuple-element.39), channel_id=1, source_target_pairs={{2,0},{4,2},{6,4},{8,6},{10,8},{12,10},{14,12},{16,14},{18,16},{20... | collective-permute-start | bytes 786440 | tf_op jit(solution)/shard_map/ppermute | solution.py:22
  30.8 14.9 %collective-permute-start.8 = (bf16[2048,128]{1,0:T(8,128)(2,1)S(1)}, bf16[2048,128]{1,0:T(8,128)(2,1)S(1)}, u32[]{:S(2)}, u32[]{:S(2)}) collective-permute-start(bf16[2048,128]{1,0:T(8,128)(2,1)S(1)} %bitcast.3), channel_id=1, source_target_pairs={{1,0},{0,1},{3,2},{2,3},{5,4},{4,5},{7,6},{6,7},{9,8},{8,9},{11,10... | collective-permute-start | bytes 1572872 | tf_op jit(solution)/shard_map/ppermute | solution.py:22
  34.9 20.5 %collective-permute-start.9 = (bf16[2048,128]{1,0:T(8,128)(2,1)S(1)}, bf16[2048,128]{1,0:T(8,128)(2,1)S(1)}, u32[]{:S(2)}, u32[]{:S(2)}) collective-permute-start(bf16[2048,128]{1,0:T(8,128)(2,1)S(1)} %bitcast.5), channel_id=1, source_target_pairs={{1,0},{0,1},{3,2},{2,3},{5,4},{4,5},{7,6},{6,7},{9,8},{8,9},{11,10... | collective-permute-start | bytes 1572872 | tf_op jit(solution)/shard_map/ppermute | solution.py:22
  56.3 1.4 %collective-permute-start.10 = (bf16[8,32,256]{2,1,0:T(8,128)(2,1)S(1)}, bf16[8,32,256]{2,1,0:T(8,128)(2,1)S(1)}, u32[]{:S(2)}, u32[]{:S(2)}) collective-permute-start(bf16[8,32,256]{2,1,0:T(8,128)(2,1)S(1)} %get-tuple-element.41), channel_id=1, source_target_pairs={{0,2},{2,0},{4,6},{6,4},{8,10},{10,8},{12,14},{14,12},{16,18},{18,... | collective-permute-start | bytes 393224 | tf_op jit(solution)/shard_map/ppermute | solution.py:283
  57.7 4.3 %collective-permute-start.11 = (bf16[4,32,256]{2,1,0:T(8,128)(2,1)S(1)}, bf16[4,32,256]{2,1,0:T(8,128)(2,1)S(1)}, u32[]{:S(2)}, u32[]{:S(2)}) collective-permute-start(bf16[4,32,256]{2,1,0:T(8,128)(2,1)S(1)} %get-tuple-element.43), channel_id=1, source_target_pairs={{0,4},{2,6},{4,0},{6,2},{8,12},{10,14},{12,8},{14,10},{16,20},{18,... | collective-permute-start | bytes 196616 | tf_op jit(solution)/shard_map/ppermute | solution.py:283
  62.1 4.0 %collective-permute-start.12 = (bf16[2,32,256]{2,1,0:T(8,128)(2,1)S(1)}, bf16[2,32,256]{2,1,0:T(8,128)(2,1)S(1)}, u32[]{:S(2)}, u32[]{:S(2)}) collective-permute-start(bf16[2,32,256]{2,1,0:T(8,128)(2,1)S(1)} %get-tuple-element.45), channel_id=1, source_target_pairs={{0,8},{2,10},{4,12},{6,14},{8,0},{10,2},{12,4},{14,6},{16,24},{18,... | collective-permute-start | bytes 98312 | tf_op jit(solution)/shard_map/ppermute | solution.py:283
  66.1 4.7 %collective-permute-start.13 = (bf16[1,32,256]{2,1,0:T(8,128)(2,1)S(1)}, bf16[1,32,256]{2,1,0:T(8,128)(2,1)S(1)}, u32[]{:S(2)}, u32[]{:S(2)}) collective-permute-start(bf16[1,32,256]{2,1,0:T(8,128)(2,1)S(1)} %get-tuple-element.47), channel_id=1, source_target_pairs={{0,16},{2,18},{4,20},{6,22},{8,24},{10,26},{12,28},{14,30},{16,0},... | collective-permute-start | bytes 49160 | tf_op jit(solution)/shard_map/ppermute | solution.py:283
